TPU v7x, 256 devices: a whole 4x4x8 slice. The times are simulated.
256 devices in a mesh: dp: 32 (over y, x, core), mp: 8 (over z).
Axes of the slice: x: 4, y: 4, z: 8, core: 2. Of those that a mesh axis runs over, the one named last changes fastest.
Arguments:
- grad_out: bfloat16 [4096, 2688], P('dp', 'mp'), may hold values from -24 to 24
- gate_pre: bfloat16 [4096, 10752], P('dp', 'mp'), may hold values from -6 to 6
- up_pre: bfloat16 [4096, 10752], P('dp', 'mp'), may hold values from -6 to 6
- down_weight: bfloat16 [2688, 10752], P('dp', 'mp'), may hold values from -0.125 to 0.125
- new_logp: float32 [4096], P('dp'), may hold values from -3 to 0
- behav_logp: float32 [4096], P('dp'), may hold values from -3 to 0
- lengths: int32 [32], P('dp'), may hold values from 1 to 128
- versions: int32 [32], P('dp'), may hold values from 0 to 7
- token_lag: int32 [4096], P('dp'), may hold values from 0 to 3
Outputs:
- d_gate: bfloat16 [4096, 10752], P('dp', 'mp')
- d_up: bfloat16 [4096, 10752], P('dp', 'mp')
- d_down: float32 [2688, 10752], P('dp', 'mp')
All inputs are finite; a program needn't handle non-finite values.
Results may differ from a plain program's by a relative error of at most 0.017.
Values may be sent and summed in bfloat16 or wider, within the bound.
A program may use at most 64 MiB of HBM per device.

v0:
```python
import functools

import jax
import jax.numpy as jnp
from jax import lax
from jax.sharding import Mesh
from jax.sharding import PartitionSpec as P

SEQ_DEV = 1
MAX_LAG = 5
NBINS = 11
DP = ("dp_0", "dp_1", "dp_2")


ratio_cap = 2.0


def sent_to_all(array, axis):
    copies = jnp.broadcast_to(array, (lax.axis_size(axis), *array.shape))
    return lax.all_to_all(copies, axis, split_axis=0, concat_axis=0, tiled=True)


def in_order(blocks, dim):
    shape = list(blocks.shape[1:])
    shape[dim] *= blocks.shape[0]
    return jnp.moveaxis(blocks, 0, dim).reshape(shape)


def gathered_copies(array, axis, dim):
    blocks = sent_to_all(array, axis)
    return in_order(blocks, dim)


def over_axes(array, axes):
    return functools.reduce(lax.psum, axes, array)


def gelu_tanh(values):
    return jax.nn.gelu(values, approximate=True)


def token_product(left, right):
    return lax.dot_general(
        left, right, (((0,), (0,)), ((), ())), preferred_element_type=jnp.float32
    )


def local(
    grad_out, gate_pre, up_pre, down_weight, new_logp, behav_logp, lengths, versions, token_lag
):
    local_tokens = token_lag.shape[0]
    local_seqs = lengths.shape[0]
    seq_len = local_tokens // local_seqs
    cotangent = gathered_copies(grad_out, "mp", 1)
    positions = jnp.arange(seq_len, dtype=jnp.int32)
    in_length = (positions[None, :] < lengths[:, None]).reshape(local_tokens)
    token_version = (versions[:, None] + token_lag.reshape(local_seqs, seq_len)).reshape(
        local_tokens
    )
    bins = jnp.arange(NBINS, dtype=jnp.int32)
    matches = (token_version[:, None] == bins[None, :]) & in_length[:, None]
    histogram = jnp.sum(matches.astype(jnp.float32), axis=0)
    totals = over_axes(histogram, DP)
    current = jnp.max(jnp.where(totals > 0, bins, -1))
    valid_count = jnp.sum(jnp.where(bins >= current - MAX_LAG, totals, jnp.float32(0.0)))
    is_valid = in_length & (token_version >= current - MAX_LAG)
    ratios = jnp.minimum(jnp.exp(new_logp - behav_logp), ratio_cap)
    weights = jnp.where(is_valid, ratios, jnp.float32(0.0)) * (
        SEQ_DEV * lax.axis_size(DP) / valid_count
    )
    scaled = (weights[:, None] * cotangent.astype(jnp.float32)).astype(jnp.bfloat16)
    gate = gate_pre.astype(jnp.float32)
    upper = up_pre.astype(jnp.float32)
    activated, slope = jax.jvp(gelu_tanh, (gate,), (jnp.ones_like(gate),))
    hidden = (activated * upper).astype(jnp.bfloat16)
    columns = scaled
    d_hidden = jnp.dot(
        columns,
        lax.all_gather(down_weight, DP, axis=0, tiled=True),
        preferred_element_type=jnp.float32,
    )
    columns = scaled
    d_down = lax.psum_scatter(
        token_product(columns, hidden).astype(jnp.bfloat16), DP, scatter_dimension=0, tiled=True
    ).astype(jnp.float32)
    d_up = (d_hidden * activated).astype(jnp.bfloat16)
    d_gate = (d_hidden * upper * slope).astype(jnp.bfloat16)
    return (d_gate, d_up, d_down)


def solution(mesh):
    split = Mesh(mesh.devices.reshape(4, 4, 2, mesh.shape["mp"]), ("dp_0", "dp_1", "dp_2", "mp"))
    placed = (P(DP, "mp"), P(DP, "mp"), P(DP, "mp"), P(DP, "mp"), P(DP), P(DP), P(DP), P(DP), P(DP))
    return jax.shard_map(
        local,
        mesh=split,
        in_specs=placed,
        out_specs=(P(DP, "mp"), P(DP, "mp"), P(DP, "mp")),
        check_vma=False,
    )
```

profile of v0, /device:TPU:1, one launch (start us, length us, event | category | flops | bytes accessed | tf_op | source)
XLA Modules:
  0.0 197.9 jit_solution(6986752932728334448)
XLA Ops:
  7.2 0.0 all-gather.3.cloned.1.call-start
  7.2 0.7 all-gather.3.cloned.1.call-update
  7.9 1.9 broadcast_in_dim.20
  9.8 9.0 %all-to-all-start = ((bf16[8,128,336]{1,2,0:T(8,128)(2,1)}), bf16[8,128,336]{1,2,0:T(8,128)(2,1)S(1)}, u32[]{:S(2)}, u32[]{:S(2)}) async-start(bf16[8,128,336]{1,2,0:T(8,128)(2,1)} %broadcast_in_dim.20), calls=%async_computation | async-start | bytes 1376256 | tf_op jit(solution)/shard_map/all_to_all | solution.py:20
  20.1 0.7 broadcast_add_fusion
  20.8 0.1 convert_reduce_fusion
  20.9 9.0 %psum.21 = f32[11]{0:T(128)S(1)} all-reduce(f32[11]{0:T(128)S(1)} %convert_reduce_fusion), channel_id=1, replica_groups=mesh['dp_0'=4,'dp_1'=4,'dp_2'=2,'mp'=8] {'dp_0'}, use_global_device_ids=true, to_apply=%region_1.0 | all-reduce | flops 11 | bytes 88 | tf_op jit(solution)/shard_map/psum | solution.py:35
  29.9 9.3 %psum.22 = f32[11]{0:T(128)S(1)} all-reduce(f32[11]{0:T(128)S(1)} %psum.21), channel_id=1, replica_groups=mesh['dp_0'=4,'dp_1'=4,'dp_2'=2,'mp'=8] {'dp_1'}, use_global_device_ids=true, to_apply=%region_2.0 | all-reduce | flops 11 | bytes 88 | tf_op jit(solution)/shard_map/psum | solution.py:35
  39.1 6.0 %psum.23 = f32[11]{0:T(128)S(1)} all-reduce(f32[11]{0:T(128)S(1)} %psum.22), channel_id=1, replica_groups=mesh['dp_0'=4,'dp_1'=4,'dp_2'=2,'mp'=8] {'dp_2'}, use_global_device_ids=true, to_apply=%region_3.0 | all-reduce | flops 11 | bytes 88 | tf_op jit(solution)/shard_map/psum | solution.py:35
  45.2 0.6 fusion.20
  46.4 0.6 fusion.21
  47.7 0.7 fusion.22
  48.4 0.0 all-to-all-done
  48.4 0.1 fusion.1
  48.6 0.0 copy-start.2
  48.6 6.4 %convolution_convert_fusion = bf16[2688,1344]{1,0:T(8,128)(2,1)} fusion(bf16[128,2688]{0,1:T(8,128)(2,1)S(1)} %fusion.1, bf16[128,1344]{0,1:T(8,128)(2,1)} %param.11, bf16[128,1344]{0,1:T(8,128)(2,1)} %param.10), kind=kOutput, calls=%fused_computation | convolution fusion | flops 930521088 | bytes 8601600 | tf_op jit(solution)/shard_map/dot_general | solution.py:43
  55.0 92.4 %fusion = bf16[96,1344]{1,0:T(8,128)(2,1)S(1)} fusion(bf16[2688,1344]{1,0:T(8,128)(2,1)} %convolution_convert_fusion), kind=kCustom, calls=%all-reduce-scatter | all-reduce-scatter fusion | flops 4128769 | bytes 7484416
  147.4 1.3 collective-permute-start.2
  148.7 1.3 collective-permute-start.1
  150.0 1.9 collective-permute-start
  151.9 0.1 slice
  152.0 1.9 collective-permute-start.3
  153.9 0.0 copy-done.2
  153.9 0.6 dynamic-slice.4
  155.2 12.4 %collective-permute-done.3 = bf16[84,1344]{1,0:T(8,128)(2,1)S(1)} collective-permute-done((bf16[84,1344]{1,0:T(8,128)(2,1)S(1)}, bf16[84,1344]{1,0:T(8,128)(2,1)S(1)}, u32[]{:S(2)}, u32[]{:S(2)}) %collective-permute-start.3) | collective-permute-done | bytes 225824
  167.5 0.0 collective-permute-done.2
  167.5 0.0 collective-permute-done.1
  167.5 0.0 collective-permute-done
  167.5 5.6 %concatenate = bf16[468,1344]{1,0:T(8,128)(2,1)S(1)} concatenate(bf16[84,1344]{1,0:T(8,128)(2,1)S(1)} %collective-permute-done.3, bf16[96,1344]{1,0:T(8,128)(2,1)S(1)} %collective-permute-done.2, bf16[96,1344]{1,0:T(8,128)(2,1)S(1)} %collective-permute-done.1, bf16[96,1344]{1,0:T(8,128)(2,1)S(1)} %collective-permute-done, bf16[96,1344]{1,0:T(8,128)(2,1)S(1)} %fusion), dimensions={0} | concatenate | bytes 2515968
  173.2 0.8 dynamic-slice_convert_fusion
  174.0 0.0 copy-start
  174.0 0.0 copy-start.1
  174.0 0.0 all-gather.3.cloned.1.call-done
  174.0 9.9 %reshape.32 = bf16[2688,1344]{1,0:T(8,128)(2,1)} reshape(bf16[32,84,1344]{2,1,0:T(8,128)(2,1)} %all-gather.3.cloned.1.call-done) | data formatting | bytes 14450688
  183.9 0.0 copy-done
  183.9 0.0 copy-done.1
  183.9 7.2 %multiply_convert_fusion = (bf16[128,1344]{0,1:T(8,128)(2,1)}, bf16[128,1344]{0,1:T(8,128)(2,1)}) fusion(bf16[128,1344]{0,1:T(8,128)(2,1)S(1)} %copy-done, bf16[128,1344]{0,1:T(8,128)(2,1)S(1)} %copy-done.1, bf16[128,2688]{0,1:T(8,128)(2,1)S(1)} %fusion.1, bf16[2688,1344]{1,0:T(8,128)(2,1)} %reshape.32), kind=kOutput, calls=%fused_computation.22 | convolution fusion | flops 928972800 | bytes 9289728 | tf_op jit(solution)/shard_map/dot_general | solution.py:77
  (1 shorter events, 0.0 us)
Async XLA Ops:
  7.2 166.9 %all-gather.3.cloned.1.call-start = ((), (), s32[]{:S(2)}) async-start(), calls=%async_computation.1 | async-start | bytes 8177664 | tf_op jit(solution)/shard_map/all_gather | solution.py:79
  9.8 38.7 %all-to-all-start = ((bf16[8,128,336]{1,2,0:T(8,128)(2,1)}), bf16[8,128,336]{1,2,0:T(8,128)(2,1)S(1)}, u32[]{:S(2)}, u32[]{:S(2)}) async-start(bf16[8,128,336]{1,2,0:T(8,128)(2,1)} %broadcast_in_dim.20), calls=%async_computation | async-start | bytes 1376256 | tf_op jit(solution)/shard_map/all_to_all | solution.py:20
  48.6 105.3 %copy-start.2 = (u32[256]{0:T(256)S(1)}, u32[256]{0:T(256)}, u32[]{:S(2)}) copy-start(u32[256]{0:T(256)} %constant.30) | copy-start | bytes 3076
  147.4 20.2 %collective-permute-start.2 = (bf16[96,1344]{1,0:T(8,128)(2,1)S(1)}, bf16[96,1344]{1,0:T(8,128)(2,1)S(1)}, u32[]{:S(2)}, u32[]{:S(2)}) collective-permute-start(bf16[96,1344]{1,0:T(8,128)(2,1)S(1)} %fusion), channel_id=1, source_target_pairs={{0,24},{8,32},{16,40},{24,48},{32,56},{40,64},{48,72},{56,80},{64,... | collective-permute-start | bytes 774152
  148.7 18.9 %collective-permute-start.1 = (bf16[96,1344]{1,0:T(8,128)(2,1)S(1)}, bf16[96,1344]{1,0:T(8,128)(2,1)S(1)}, u32[]{:S(2)}, u32[]{:S(2)}) collective-permute-start(bf16[96,1344]{1,0:T(8,128)(2,1)S(1)} %fusion), channel_id=1, source_target_pairs={{0,16},{8,24},{16,32},{24,40},{32,48},{40,56},{48,64},{56,72},{64,... | collective-permute-start | bytes 774152
  150.0 17.5 %collective-permute-start = (bf16[96,1344]{1,0:T(8,128)(2,1)S(1)}, bf16[96,1344]{1,0:T(8,128)(2,1)S(1)}, u32[]{:S(2)}, u32[]{:S(2)}) collective-permute-start(bf16[96,1344]{1,0:T(8,128)(2,1)S(1)} %fusion), channel_id=1, source_target_pairs={{0,8},{8,16},{16,24},{24,32},{32,40},{40,48},{48,56},{56,64},{64,7... | collective-permute-start | bytes 774152
  152.0 15.5 %collective-permute-start.3 = (bf16[84,1344]{1,0:T(8,128)(2,1)S(1)}, bf16[84,1344]{1,0:T(8,128)(2,1)S(1)}, u32[]{:S(2)}, u32[]{:S(2)}) collective-permute-start(bf16[84,1344]{1,0:T(8,128)(2,1)S(1)} %slice), channel_id=1, source_target_pairs={{0,32},{8,40},{16,48},{24,56},{32,64},{40,72},{48,80},{56,88},{64,... | collective-permute-start | bytes 677384
  174.0 9.9 %copy-start = (bf16[128,1344]{0,1:T(8,128)(2,1)S(1)}, bf16[128,1344]{0,1:T(8,128)(2,1)}, u32[]{:S(2)}) copy-start(bf16[128,1344]{0,1:T(8,128)(2,1)} %param.10) | copy-start | bytes 1032196
  174.0 9.9 %copy-start.1 = (bf16[128,1344]{0,1:T(8,128)(2,1)S(1)}, bf16[128,1344]{0,1:T(8,128)(2,1)}, u32[]{:S(2)}) copy-start(bf16[128,1344]{0,1:T(8,128)(2,1)} %param.11) | copy-start | bytes 1032196
Sparse Core Ops, SparseCore 0:
  10.6 65.6 all-gather.2
where the time goes:
time: 200 us; the launch traced here: 198 us
  blocking collectives  117 us (58%)
  local copies, waits for them, and re-layouts  18 us (9%)
  between operations  17.4 us (9%)
  starting transfers between devices  15.5 us (8%)
  matrix products  13.6 us (7%)
  waiting for transfers between devices  13.1 us (7%)
  other arithmetic  3.7 us (2%)
    unnamed x1, blocking collectives  92.4 us
    psum x3, blocking collectives, over_axes(): return functools.reduce(lax.psum, axes, array)  24.3 us
    unnamed x10, local copies, waits for them, and re-layouts  16.2 us
    unnamed x5, waiting for transfers between devices  13.1 us
    all_to_all x1, starting transfers between devices, sent_to_all(): return lax.all_to_all(copies, axis, split_axis=0, concat_axis=0, tiled=True)  9 us
    dot_general x1, matrix products, local(): jnp.dot(columns, lax.all_gather(down_weight, DP, axis=0, tiled=True), pre...  7.2 us
    unnamed x4, starting transfers between devices  6.45 us
    dot_general x1, matrix products, token_product(): lax.dot_general(left, right, (((0,), (0,)), ((), ())), preferred_element_...  6.35 us
  transfers between devices with their start and end apart: 6, of which 1 were waited for; matrix products, arithmetic and copies ran while one was open for 56% of the time, Pallas kernels for 0%

commit v1 on v0

v1 whole, which is shorter than its diff:
```python
import functools
import math

import jax
import jax.numpy as jnp
from jax import lax
from jax.experimental import pallas as pl
from jax.experimental.pallas import tpu as pltpu
from jax.sharding import Mesh
from jax.sharding import PartitionSpec as P

MAX_LAG = 5
DP = ("dp_0", "dp_1", "dp_2")
MESH = pl.DeviceIdType.MESH
F32, BF16 = jnp.float32, jnp.bfloat16
RATIO_CAP = 2.0
ROOT = math.sqrt(2.0 / math.pi)
CUBIC = 0.044715


def kernel(
    rows, low, weight, cotangent, gate, up, new_logp, old_logp, lag, length, version,
    d_gate, d_up, d_down,
    weights_all, cot_all, cot_mine, hidden, gate_v, up_v, act, up_slope, parts, others, acc, acc_in, hist_out, hist_in,
    partial, far_out, full_out, half_in, full_in, far_out1, full_out1, half_in1, full_in1, gate_out, up_out, down_out,
    copy_sem, out_sem, hist_send, hist_recv, z_send, z_recv, ag_send, ag_recv, core_send, core_recv,
    a_send, f_send, h_recv, f_recv, a1_send, f1_send, h1_recv, f1_recv,
):
    y, x, c, z = (lax.axis_index(name) for name in (*DP, "mp"))
    tokens = hidden.shape[0] // 2
    lo, hi = pl.ds(0, low), pl.ds(low, rows - low)

    def at(i, j):
        return (
            lax.rem(y + 4 + i * c + j * (1 - c), 4),
            lax.rem(x + 4 + i * (1 - c) + j * c, 4),
        )

    def device(i, j):
        yy, xx = at(i, j)
        return (yy, xx, c, z)

    def block(i, j):
        yy, xx = at(i, j)
        return yy * 4 + xx

    twin = (y, x, 1 - c, z)
    z_peers = [(y, x, c, lax.rem(z + d, 8)) for d in range(1, 8)]
    x_peers = [(y, lax.rem(x + d, 4), c, z) for d in range(1, 4)]
    y_peers = [(lax.rem(y + d, 4), x, c, z) for d in range(1, 4)]
    peers = [twin, *z_peers, *x_peers, *y_peers]

    def remote(src, dst, send, recv, to):
        return pltpu.make_async_remote_copy(
            src_ref=src, dst_ref=dst, send_sem=send, recv_sem=recv, device_id=to, device_id_type=MESH
        )

    barrier = pltpu.get_barrier_semaphore()
    for peer in peers:
        pl.semaphore_signal(barrier, inc=1, device_id=peer, device_id_type=MESH)

    own = block(0, 0)
    local = [
        pltpu.make_async_copy(gate, gate_v, copy_sem.at[0]),
        pltpu.make_async_copy(up, up_v, copy_sem.at[1]),
        pltpu.make_async_copy(cotangent, cot_mine, copy_sem.at[2]),
        pltpu.make_async_copy(weight, weights_all.at[own], copy_sem.at[3]),
    ]
    for copy in local:
        copy.start()

    bins = lax.broadcasted_iota(jnp.int32, (16, tokens), 0)
    position = lax.broadcasted_iota(jnp.int32, (1, tokens), 1)
    live = position < length[0]
    token_version = lag[...] + version[0]
    match = jnp.where((token_version == bins) & live, 1.0, 0.0)
    counts = jnp.broadcast_to(jnp.sum(match, axis=1, keepdims=True), (16, tokens))
    hist_out[0] = counts

    pl.semaphore_wait(barrier, len(peers))

    sent = []

    def go(copy):
        copy.start()
        sent.append(copy)

    for d in range(3):
        go(remote(hist_out.at[0], hist_in.at[d], hist_send.at[d], hist_recv.at[d], x_peers[d]))

    fulls = {(-1, 0): 0, (1, 0): 1, (0, -1): 2, (0, 1): 3, (-1, -1): 4, (-1, 1): 5, (1, -1): 6, (1, 1): 7, (2, -1): 8, (2, 1): 9}
    halves = {(2, 0): 10, (0, 2): 12, (-1, 2): 14, (1, 2): 16, (2, 2): 18}
    steps = {0: (1, 0), 1: (-1, 0), 2: (0, 1), 3: (0, -1)}

    def forward(i, j, way, half=None, src=None):
        di, dj = steps[way]
        slot = weights_all.at[block(i, j)]
        ni, nj = i - di, j - dj
        if half is None:
            sem = fulls[(ni, nj)]
            part = slot
        else:
            ni, nj = (2 if ni in (-2, 2) else ni), (2 if nj in (-2, 2) else nj)
            sem = halves[(ni, nj)] + half
            part = slot.at[lo if half == 0 else hi]
        go(remote(part if src is None else src, part, ag_send.at[len(used)], ag_recv.at[sem], device(di, dj)))
        used.append(sem)

    used = []

    def landed(i, j, half=None):
        slot = weights_all.at[block(i, j)]
        if half is None:
            sem, part = fulls[(i, j)], slot
        else:
            sem, part = halves[(i, j)] + half, slot.at[lo if half == 0 else hi]
        remote(part, part, ag_send.at[0], ag_recv.at[sem], twin).wait_recv()

    for way in range(4):
        forward(0, 0, way, src=weight)
    for d in range(7):
        go(remote(cotangent, cot_all.at[d], z_send.at[d], z_recv.at[d], z_peers[d]))

    local[0].wait()
    local[1].wait()

    def elementwise(n, carry):
        at_rows = pl.ds(pl.multiple_of(n * 16, 16), 16)
        v = gate_v[at_rows].astype(F32)
        u = up_v[at_rows].astype(F32)
        square = v * v
        t = jnp.tanh(ROOT * (v + CUBIC * (square * v)))
        half = 0.5 * (1.0 + t)
        a = v * half
        slope = half + (0.5 * v) * (1.0 - t * t) * (ROOT * (1.0 + (3.0 * CUBIC) * square))
        act[at_rows] = a
        up_slope[at_rows] = u * slope
        hidden[at_rows] = (a * u).astype(BF16)
        return carry

    lax.fori_loop(0, tokens // 16, elementwise, 0)
    mine, theirs = pl.ds(0, tokens), pl.ds(tokens, tokens)
    swap_hidden = remote(hidden.at[mine], hidden.at[theirs], core_send.at[0], core_recv.at[0], twin)
    swap_hidden.start()

    def received(n):
        remote(hist_in.at[n], hist_in.at[n], hist_send.at[n], hist_recv.at[n], twin).wait_recv()
        return hist_in[n]

    counts = counts + received(0) + received(1) + received(2)
    hist_out[1] = counts
    for d in range(3):
        go(remote(hist_out.at[1], hist_in.at[3 + d], hist_send.at[3 + d], hist_recv.at[3 + d], y_peers[d]))

    for i in (-1, 1):
        landed(i, 0)
        forward(i, 0, 0 if i == -1 else 1, half=0 if i == -1 else 1)
        forward(i, 0, 2)
        forward(i, 0, 3)

    counts = counts + received(3) + received(4) + received(5)
    hist_out[2] = counts
    go(remote(hist_out.at[2], hist_in.at[6], hist_send.at[6], hist_recv.at[6], twin))

    def pass_on(i):
        landed(i, -1)
        forward(i, -1, 2, half=0)
        landed(i, 1)
        forward(i, 1, 3, half=1)

    pass_on(0)
    landed(2, 0, 0)
    landed(2, 0, 1)
    forward(2, 0, 2)
    forward(2, 0, 3)

    counts = counts + received(6)
    current = jnp.max(jnp.where(counts > 0, bins, -1), axis=0, keepdims=True)
    oldest = current - MAX_LAG
    valid_count = jnp.sum(jnp.where(bins >= oldest, counts, 0.0), axis=0, keepdims=True)
    valid = live & (token_version >= oldest)
    ratio = jnp.minimum(jnp.exp(new_logp[...] - old_logp[...]), RATIO_CAP)
    token_weight = jnp.where(valid, ratio, 0.0) * (32.0 / valid_count)
    row_id = lax.broadcasted_iota(jnp.int32, (tokens, tokens), 0)
    lane_id = lax.broadcasted_iota(jnp.int32, (tokens, tokens), 1)
    column = jnp.sum(jnp.where(row_id == lane_id, token_weight, 0.0), axis=1, keepdims=True)

    width = cotangent.shape[1]
    source = lax.broadcasted_iota(jnp.int32, (width, 512), 0)
    target = lax.broadcasted_iota(jnp.int32, (width, 512), 1)
    lane = target & 127
    group = target >> 7
    parity = jnp.where(group < 2, c, 1 - c)
    wanted = rows * (2 * (group & 1) + parity) + lane
    select = jnp.where((source == wanted) & (lane < rows), 1.0, 0.0).astype(BF16)

    def place(values, owner):
        scaled = (column * values.astype(F32)).astype(BF16)
        picked = jnp.dot(scaled, select, preferred_element_type=F32).astype(BF16)
        for k in range(2):
            parts[2 * owner + k, pl.ds(0, tokens), :] = picked[:, k * 128 : (k + 1) * 128]
            others[2 * owner + k] = picked[:, (k + 2) * 128 : (k + 3) * 128]

    local[2].wait()
    place(cot_mine[...], z)
    pass_on(-1)
    pass_on(1)

    def place_from(d, carry):
        remote(cot_all.at[d], cot_all.at[d], z_send.at[d], z_recv.at[d], twin).wait_recv()
        place(cot_all[d], lax.rem(z + 7 - d, 8))
        return carry

    lax.fori_loop(0, 7, place_from, 0)
    swap_parts = remote(others, parts.at[:, theirs], core_send.at[1], core_recv.at[1], twin)
    swap_parts.start()
    pass_on(2)
    swap_hidden.wait()
    swap_parts.wait_recv()

    def product(p):
        return lax.dot_general(
            parts[p], hidden[...], (((0,), (0,)), ((), ())), preferred_element_type=F32
        )[:rows]

    def offset(n):
        return jnp.where(n < 2, n + 2, 3 - n)

    def start_far(n, carry):
        far_out[n] = product(block(offset(n), 2)).astype(BF16)
        remote(far_out.at[n, lo], half_in.at[n, lo], a_send.at[n, 0], h_recv.at[n, 0], device(0, 1)).start()
        remote(far_out.at[n, hi], half_in.at[n, hi], a_send.at[n, 1], h_recv.at[n, 1], device(0, -1)).start()
        return carry

    lax.fori_loop(0, 4, start_far, 0)

    def rest(t, carry):
        n, m = t // 3, lax.rem(t, 3)
        partial[n, m] = product(block(offset(n), jnp.where(m == 0, 1, jnp.where(m == 1, 3, 0))))
        return carry

    lax.fori_loop(0, 12, rest, 0)

    for i in (0, -1, 1, 2):
        landed(i, 2, 0)
        landed(i, 2, 1)
    local[3].wait()
    acc[...] = jnp.zeros_like(acc)

    def accumulate(p, carry):
        acc[...] += jnp.dot(parts[p][:, :rows], weights_all[p], preferred_element_type=F32)
        return carry

    lax.fori_loop(0, 16, accumulate, 0)
    swap_acc = remote(acc.at[theirs], acc_in, core_send.at[2], core_recv.at[2], twin)
    swap_acc.start()

    def pass_full(n, carry):
        for side, (part, way) in enumerate(((lo, 1), (hi, -1))):
            remote(half_in.at[n, part], half_in.at[n, part], a_send.at[n, side], h_recv.at[n, side], twin).wait_recv()
            first = partial[n, side, lo]
            second = partial[n, side, hi]
            arrived = half_in[n, part].astype(F32)
            if side == 0:
                first = first + arrived
            else:
                second = second + arrived
            full_out[n, side, lo] = first.astype(BF16)
            full_out[n, side, hi] = second.astype(BF16)
            remote(full_out.at[n, side], full_in.at[n, side], f_send.at[n, side], f_recv.at[n, side], device(0, way)).start()
        return carry

    lax.fori_loop(0, 4, pass_full, 0)

    swap_acc.wait_recv()
    outs = []

    def finish(n, carry):
        at_rows = pl.ds(pl.multiple_of(n * 16, 16), 16)
        total = acc[at_rows] + acc_in[at_rows]
        up_out[at_rows] = (total * act[at_rows]).astype(BF16)
        gate_out[at_rows] = (total * up_slope[at_rows]).astype(BF16)
        return carry

    lax.fori_loop(0, tokens // 16, finish, 0)
    for n, (src, dst) in enumerate(((gate_out, d_gate), (up_out, d_up))):
        outs.append(pltpu.make_async_copy(src, dst, out_sem.at[n]))
        outs[-1].start()

    def ring_sum(n):
        for side in range(2):
            remote(full_in.at[n, side], full_in.at[n, side], f_send.at[n, side], f_recv.at[n, side], twin).wait_recv()
        return partial[n, 2] + full_in[n, 0].astype(F32) + full_in[n, 1].astype(F32)

    far_out1[...] = ring_sum(0).astype(BF16)
    far = [
        remote(far_out1.at[part], half_in1.at[part], a1_send.at[side], h1_recv.at[side], device(way, 0))
        for side, (part, way) in enumerate(((lo, 1), (hi, -1)))
    ]
    for copy in far:
        copy.start()
    full1 = []
    for n, side in ((1, 1), (2, 0)):
        down_out[...] = ring_sum(n)
        part, way = ((lo, 1), (hi, -1))[side]
        far[side].wait_recv()
        down_out[part] += half_in1[part].astype(F32)
        full_out1[side] = down_out[...].astype(BF16)
        full1.append(
            remote(full_out1.at[side], full_in1.at[side], f1_send.at[side], f1_recv.at[side], device(way, 0))
        )
        full1[-1].start()
    down_out[...] = ring_sum(3)
    for copy in full1:
        copy.wait_recv()
    down_out[...] += full_in1[0].astype(F32) + full_in1[1].astype(F32)
    outs.append(pltpu.make_async_copy(down_out, d_down, out_sem.at[2]))
    outs[-1].start()

    for copy in (*sent, *far, *full1, swap_parts, swap_acc):
        copy.wait_send()

    def drain(n, carry):
        for side, part in enumerate((lo, hi)):
            remote(far_out.at[n, part], half_in.at[n, part], a_send.at[n, side], h_recv.at[n, side], twin).wait_send()
            remote(full_out.at[n, side], full_in.at[n, side], f_send.at[n, side], f_recv.at[n, side], twin).wait_send()
        return carry

    lax.fori_loop(0, 4, drain, 0)
    for copy in outs:
        copy.wait()


def local(grad_out, gate_pre, up_pre, down_weight, new_logp, behav_logp, lengths, versions, token_lag):
    tokens, ff = gate_pre.shape
    rows = down_weight.shape[0]
    width = grad_out.shape[1]
    low = 40
    hbm = pl.BlockSpec(memory_space=pl.ANY)
    vmem = pl.BlockSpec(memory_space=pltpu.VMEM)
    smem = pl.BlockSpec(memory_space=pltpu.SMEM)
    dma = pltpu.SemaphoreType.DMA

    def line(values):
        return values.reshape(1, tokens)

    scratch = [
        pltpu.VMEM((16, rows, ff), BF16),
        pltpu.VMEM((7, tokens, width), BF16),
        pltpu.VMEM((tokens, width), BF16),
        pltpu.VMEM((2 * tokens, ff), BF16),
        pltpu.VMEM((tokens, ff), BF16),
        pltpu.VMEM((tokens, ff), BF16),
        pltpu.VMEM((tokens, ff), F32),
        pltpu.VMEM((tokens, ff), F32),
        pltpu.VMEM((16, 2 * tokens, 128), BF16),
        pltpu.VMEM((16, tokens, 128), BF16),
        pltpu.VMEM((2 * tokens, ff), F32),
        pltpu.VMEM((tokens, ff), F32),
        pltpu.VMEM((3, 16, tokens), F32),
        pltpu.VMEM((7, 16, tokens), F32),
        pltpu.VMEM((4, 3, rows, ff), F32),
        pltpu.VMEM((4, rows, ff), BF16),
        pltpu.VMEM((4, 2, rows, ff), BF16),
        pltpu.VMEM((4, rows, ff), BF16),
        pltpu.VMEM((4, 2, rows, ff), BF16),
        pltpu.VMEM((rows, ff), BF16),
        pltpu.VMEM((2, rows, ff), BF16),
        pltpu.VMEM((rows, ff), BF16),
        pltpu.VMEM((2, rows, ff), BF16),
        pltpu.VMEM((tokens, ff), BF16),
        pltpu.VMEM((tokens, ff), BF16),
        pltpu.VMEM((rows, ff), F32),
        dma((4,)), dma((3,)), dma((7,)), dma((7,)), dma((7,)), dma((7,)), dma((20,)), dma((20,)), dma((3,)), dma((3,)),
        dma((4, 2)), dma((4, 2)), dma((4, 2)), dma((4, 2)), dma((2,)), dma((2,)), dma((2,)), dma((2,)),
    ]
    return pl.pallas_call(
        functools.partial(kernel, rows, low),
        out_shape=(
            jax.ShapeDtypeStruct((tokens, ff), BF16),
            jax.ShapeDtypeStruct((tokens, ff), BF16),
            jax.ShapeDtypeStruct((rows, ff), F32),
        ),
        in_specs=[hbm, hbm, hbm, hbm, vmem, vmem, vmem, smem, smem],
        out_specs=(hbm, hbm, hbm),
        scratch_shapes=scratch,
        compiler_params=pltpu.CompilerParams(
            collective_id=0, has_side_effects=True, vmem_limit_bytes=60 * 1024 * 1024
        ),
    )(
        down_weight, grad_out, gate_pre, up_pre, line(new_logp), line(behav_logp), line(token_lag), lengths, versions
    )


def solution(mesh):
    split = Mesh(mesh.devices.reshape(4, 4, 2, mesh.shape["mp"]), (*DP, "mp"))
    placed = (P(DP, "mp"), P(DP, "mp"), P(DP, "mp"), P(DP, "mp"), P(DP), P(DP), P(DP), P(DP), P(DP))
    return jax.shard_map(
        local,
        mesh=split,
        in_specs=placed,
        out_specs=(P(DP, "mp"), P(DP, "mp"), P(DP, "mp")),
        check_vma=False,
    )
```

time: 200 us -> 72.1 us (0.36)
  blocking collectives: 117 us -> 0 us
  Pallas kernels: 0 us -> 61.7 us
  starting transfers between devices: 15.5 us -> 0 us
  between operations: 17.4 us -> 1.94 us
  matrix products: 13.6 us -> 0 us
  waiting for transfers between devices: 13.1 us -> 0 us
  local copies, waits for them, and re-layouts: 18 us -> 8.24 us
  other arithmetic: 3.7 us -> 0 us
    unnamed x1 -> x0, blocking collectives: 92.4 us -> none
    pallas_call x0 -> x1, Pallas kernels: none -> 61.7 us  [local(): pl.pallas_call(functools.partial(kernel, rows, low), out_shape=(jax.Shape...]
    psum x3 -> x0, blocking collectives: 24.3 us -> none  [over_axes(): return functools.reduce(lax.psum, axes, array)]
    dot_general x2 -> x0, matrix products: 13.6 us -> none  [the longest x1 7.2 us: local(): jnp.dot(columns, lax.all_gather(down_weight, DP, axis=0, tiled=True), pre...]
    unnamed x5 -> x0, waiting for transfers between devices: 13.1 us -> none
    unnamed x10, local copies, waits for them, and re-layouts: 16.2 us -> 5.39 us
    all_to_all x1 -> x0, starting transfers between devices: 9 us -> none  [sent_to_all(): return lax.all_to_all(copies, axis, split_axis=0, concat_axis=0, tiled=True)]
    unnamed x4 -> x0, starting transfers between devices: 6.45 us -> none
  transfers between devices with their start and end apart: 6 -> 0, of which waited for: 1 -> 0; matrix products, arithmetic and copies ran while one was open for 56% -> 0% of each run, Pallas kernels for 0% -> 0%
where the time goes in v1:
time: 72.1 us; the launch traced here: 71.9 us
  Pallas kernels  61.7 us (86%)
  local copies, waits for them, and re-layouts  8.24 us (11%)
  between operations  1.94 us (3%)
    pallas_call x1, Pallas kernels, local(): pl.pallas_call(functools.partial(kernel, rows, low), out_shape=(jax.Shape...  61.7 us
    unnamed x10, local copies, waits for them, and re-layouts  5.39 us
    pallas_call x2, local copies, waits for them, and re-layouts, local(): pl.pallas_call(functools.partial(kernel, rows, low), out_shape=(jax.Shape...  2.85 us

profile of v1, /device:TPU:1, one launch (start us, length us, event | category | flops | bytes accessed | tf_op | source)
XLA Modules:
  0.0 71.9 jit_solution(18311611232140343098)
XLA Ops:
  1.9 1.6 %copy.12.cotangent = bf16[128,336]{1,0:T(8,128)(2,1)} copy(bf16[128,336]{0,1:T(8,128)(2,1)} %param.9) | data formatting | bytes 172032 | tf_op args[0]
  3.6 0.0 copy-start.2
  3.6 1.9 %copy.13.gate = bf16[128,1344]{1,0:T(8,128)(2,1)} copy(bf16[128,1344]{0,1:T(8,128)(2,1)} %param.10) | data formatting | bytes 688128 | tf_op args[1]
  5.5 0.0 copy-done.2
  5.5 0.9 %copy.14.up = bf16[128,1344]{1,0:T(8,128)(2,1)} copy(bf16[128,1344]{0,1:T(8,128)(2,1)S(1)} %copy-done.2) | data formatting | bytes 688128 | tf_op args[2]
  6.4 61.7 %shard_map.112 = (bf16[128,1344]{1,0:T(8,128)(2,1)}, bf16[128,1344]{1,0:T(8,128)(2,1)}, f32[84,1344]{1,0:T(8,128)}) custom-call(bf16[84,1344]{1,0:T(8,128)(2,1)} %weight.1, bf16[128,336]{1,0:T(8,128)(2,1)} %copy.12.cotangent, bf16[128,1344]{1,0:T(8,128)(2,1)} %copy.13.gate, bf16[128,1344]{1,0:T(8,128)(2,1)} %copy.14.up, f32[1,128]{1,0:T(1,128)} %bitcast.3, ...), custom_call_target="tpu_custom_call" | custom-call | tf_op jit(solution)/shard_map/pallas_call | solution.py:377
  68.1 0.0 copy-start.1
  68.1 1.9 %copy.15 = bf16[128,1344]{0,1:T(8,128)(2,1)} copy(bf16[128,1344]{1,0:T(8,128)(2,1)} %get-tuple-element.3) | data formatting | bytes 688128 | tf_op jit(solution)/shard_map/pallas_call | solution.py:377
  70.1 0.0 copy-done.1
  70.1 0.0 copy-start
  70.1 0.9 %copy.16 = bf16[128,1344]{0,1:T(8,128)(2,1)} copy(bf16[128,1344]{1,0:T(8,128)(2,1)S(1)} %copy-done.1) | data formatting | bytes 688128 | tf_op jit(solution)/shard_map/pallas_call | solution.py:377
  71.0 0.1 copy-done
  71.1 0.8 %copy.20 = f32[84,1344]{1,0:T(8,128)} copy(f32[84,1344]{1,0:T(8,128)S(1)} %copy-done) | data formatting | bytes 903168
Async XLA Ops:
  3.6 1.9 %copy-start.2 = (bf16[128,1344]{0,1:T(8,128)(2,1)S(1)}, bf16[128,1344]{0,1:T(8,128)(2,1)}, u32[]{:S(2)}) copy-start(bf16[128,1344]{0,1:T(8,128)(2,1)} %param.11) | copy-start | bytes 1032196
  68.1 1.9 %copy-start.1 = (bf16[128,1344]{1,0:T(8,128)(2,1)S(1)}, bf16[128,1344]{1,0:T(8,128)(2,1)}, u32[]{:S(2)}) copy-start(bf16[128,1344]{1,0:T(8,128)(2,1)} %get-tuple-element.4) | copy-start | bytes 1032196
  70.1 1.0 %copy-start = (f32[84,1344]{1,0:T(8,128)S(1)}, f32[84,1344]{1,0:T(8,128)}, u32[]{:S(2)}) copy-start(f32[84,1344]{1,0:T(8,128)} %get-tuple-element.11) | copy-start | bytes 1354756

commit v2 on v1

--- a/solution.py
+++ b/solution.py
@@ -21,13 +21,14 @@
 def kernel(
     rows, low, weight, cotangent, gate, up, new_logp, old_logp, lag, length, version,
     d_gate, d_up, d_down,
-    weights_all, cot_all, cot_mine, hidden, gate_v, up_v, act, up_slope, parts, others, acc, acc_in, hist_out, hist_in,
+    weights_all, cot_all, hidden, gate_v, up_v, act, up_slope, parts, others, acc, acc_in, hist_out, hist_in,
+    new_v, old_v, lag_v,
     partial, far_out, full_out, half_in, full_in, far_out1, full_out1, half_in1, full_in1, gate_out, up_out, down_out,
     copy_sem, out_sem, hist_send, hist_recv, z_send, z_recv, ag_send, ag_recv, core_send, core_recv,
     a_send, f_send, h_recv, f_recv, a1_send, f1_send, h1_recv, f1_recv,
 ):
     y, x, c, z = (lax.axis_index(name) for name in (*DP, "mp"))
-    tokens = hidden.shape[0] // 2
+    tokens, units = hidden.shape[0] // 2, hidden.shape[1]
     lo, hi = pl.ds(0, low), pl.ds(low, rows - low)
 
     def at(i, j):
@@ -45,10 +46,10 @@
         return yy * 4 + xx
 
     twin = (y, x, 1 - c, z)
-    z_peers = [(y, x, c, lax.rem(z + d, 8)) for d in range(1, 8)]
+    z_peers = {d: (y, x, c, lax.rem(z + 8 + d, 8)) for d in (-2, 2, -1, 1)}
     x_peers = [(y, lax.rem(x + d, 4), c, z) for d in range(1, 4)]
     y_peers = [(lax.rem(y + d, 4), x, c, z) for d in range(1, 4)]
-    peers = [twin, *z_peers, *x_peers, *y_peers]
+    peers = [twin, *z_peers.values(), *x_peers, *y_peers]
 
     def remote(src, dst, send, recv, to):
         return pltpu.make_async_remote_copy(
@@ -63,16 +64,22 @@
     local = [
         pltpu.make_async_copy(gate, gate_v, copy_sem.at[0]),
         pltpu.make_async_copy(up, up_v, copy_sem.at[1]),
-        pltpu.make_async_copy(cotangent, cot_mine, copy_sem.at[2]),
+        pltpu.make_async_copy(cotangent, cot_all.at[0], copy_sem.at[2]),
         pltpu.make_async_copy(weight, weights_all.at[own], copy_sem.at[3]),
     ]
-    for copy in local:
+    small = [
+        pltpu.make_async_copy(src, dst, copy_sem.at[4 + n])
+        for n, (src, dst) in enumerate(((lag, lag_v), (new_logp, new_v), (old_logp, old_v)))
+    ]
+    for copy in (*small, *local):
         copy.start()
+    for copy in small:
+        copy.wait()
 
     bins = lax.broadcasted_iota(jnp.int32, (16, tokens), 0)
     position = lax.broadcasted_iota(jnp.int32, (1, tokens), 1)
     live = position < length[0]
-    token_version = lag[...] + version[0]
+    token_version = lag_v[...] + version[0]
     match = jnp.where((token_version == bins) & live, 1.0, 0.0)
     counts = jnp.broadcast_to(jnp.sum(match, axis=1, keepdims=True), (16, tokens))
     hist_out[0] = counts
@@ -118,27 +125,43 @@
 
     for way in range(4):
         forward(0, 0, way, src=weight)
-    for d in range(7):
-        go(remote(cotangent, cot_all.at[d], z_send.at[d], z_recv.at[d], z_peers[d]))
+    width = cotangent.shape[0]
+    front, back = pl.ds(0, width // 2), pl.ds(width // 2, width // 2)
+
+    def z_wait(d, half=None):
+        part = cot_all.at[d] if half is None else cot_all.at[d, (front, back)[half]]
+        sem = d - 1 if half is None else (3, 7)[half]
+        remote(part, part, z_send.at[0], z_recv.at[sem], twin).wait_recv()
+
+    for n, (d, slot) in enumerate(((2, 2), (-2, 6), (1, 1), (-1, 7))):
+        go(remote(cotangent, cot_all.at[slot], z_send.at[n], z_recv.at[slot - 1], z_peers[d]))
 
     local[0].wait()
     local[1].wait()
 
-    def elementwise(n, carry):
-        at_rows = pl.ds(pl.multiple_of(n * 16, 16), 16)
-        v = gate_v[at_rows].astype(F32)
-        u = up_v[at_rows].astype(F32)
+    def elementwise(start, size):
+        here = pl.ds(start, size)
+        v = gate_v[here].astype(F32)
+        u = up_v[here].astype(F32)
         square = v * v
         t = jnp.tanh(ROOT * (v + CUBIC * (square * v)))
         half = 0.5 * (1.0 + t)
         a = v * half
         slope = half + (0.5 * v) * (1.0 - t * t) * (ROOT * (1.0 + (3.0 * CUBIC) * square))
-        act[at_rows] = a
-        up_slope[at_rows] = u * slope
-        hidden[at_rows] = (a * u).astype(BF16)
-        return carry
-
-    lax.fori_loop(0, tokens // 16, elementwise, 0)
+        act[here] = a
+        up_slope[here] = u * slope
+        hidden[pl.ds(0, tokens), here] = (a * u).T.astype(BF16)
+
+    def over_units(body):
+        def step(n, carry):
+            body(pl.multiple_of(n * 128, 128), 128)
+            return carry
+
+        lax.fori_loop(0, units // 128, step, 0)
+        if units % 128:
+            body(units // 128 * 128, units % 128)
+
+    over_units(elementwise)
     mine, theirs = pl.ds(0, tokens), pl.ds(tokens, tokens)
     swap_hidden = remote(hidden.at[mine], hidden.at[theirs], core_send.at[0], core_recv.at[0], twin)
     swap_hidden.start()
@@ -151,6 +174,13 @@
     hist_out[1] = counts
     for d in range(3):
         go(remote(hist_out.at[1], hist_in.at[3 + d], hist_send.at[3 + d], hist_recv.at[3 + d], y_peers[d]))
+
+    z_wait(2)
+    go(remote(cot_all.at[2], cot_all.at[3], z_send.at[4], z_recv.at[2], z_peers[1]))
+    go(remote(cot_all.at[2, front], cot_all.at[4, front], z_send.at[5], z_recv.at[3], z_peers[2]))
+    z_wait(6)
+    go(remote(cot_all.at[6], cot_all.at[5], z_send.at[6], z_recv.at[4], z_peers[-1]))
+    go(remote(cot_all.at[6, back], cot_all.at[4, back], z_send.at[7], z_recv.at[7], z_peers[-2]))
 
     for i in (-1, 1):
         landed(i, 0)
@@ -168,60 +198,57 @@
         landed(i, 1)
         forward(i, 1, 3, half=1)
 
-    pass_on(0)
-    landed(2, 0, 0)
-    landed(2, 0, 1)
-    forward(2, 0, 2)
-    forward(2, 0, 3)
-
     counts = counts + received(6)
     current = jnp.max(jnp.where(counts > 0, bins, -1), axis=0, keepdims=True)
     oldest = current - MAX_LAG
     valid_count = jnp.sum(jnp.where(bins >= oldest, counts, 0.0), axis=0, keepdims=True)
     valid = live & (token_version >= oldest)
-    ratio = jnp.minimum(jnp.exp(new_logp[...] - old_logp[...]), RATIO_CAP)
+    ratio = jnp.minimum(jnp.exp(new_v[...] - old_v[...]), RATIO_CAP)
     token_weight = jnp.where(valid, ratio, 0.0) * (32.0 / valid_count)
-    row_id = lax.broadcasted_iota(jnp.int32, (tokens, tokens), 0)
-    lane_id = lax.broadcasted_iota(jnp.int32, (tokens, tokens), 1)
-    column = jnp.sum(jnp.where(row_id == lane_id, token_weight, 0.0), axis=1, keepdims=True)
-
-    width = cotangent.shape[1]
-    source = lax.broadcasted_iota(jnp.int32, (width, 512), 0)
-    target = lax.broadcasted_iota(jnp.int32, (width, 512), 1)
-    lane = target & 127
-    group = target >> 7
+
+    tall = parts.shape[1]
+    line = lax.broadcasted_iota(jnp.int32, (4 * tall, width), 0)
+    source = lax.broadcasted_iota(jnp.int32, (4 * tall, width), 1)
+    group = (line >= tall).astype(jnp.int32) + (line >= 2 * tall).astype(jnp.int32) + (line >= 3 * tall).astype(jnp.int32)
+    row = line - tall * group
     parity = jnp.where(group < 2, c, 1 - c)
-    wanted = rows * (2 * (group & 1) + parity) + lane
-    select = jnp.where((source == wanted) & (lane < rows), 1.0, 0.0).astype(BF16)
-
-    def place(values, owner):
-        scaled = (column * values.astype(F32)).astype(BF16)
-        picked = jnp.dot(scaled, select, preferred_element_type=F32).astype(BF16)
+    wanted = rows * (2 * (group & 1) + parity) + row
+    select = jnp.where((source == wanted) & (row < rows), 1.0, 0.0).astype(BF16)
+
+    def place(d):
+        owner = lax.rem(z + 8 - d, 8)
+        scaled = (token_weight * cot_all[d].astype(F32)).astype(BF16)
+        picked = jnp.dot(select, scaled, preferred_element_type=F32).astype(BF16)
         for k in range(2):
-            parts[2 * owner + k, pl.ds(0, tokens), :] = picked[:, k * 128 : (k + 1) * 128]
-            others[2 * owner + k] = picked[:, (k + 2) * 128 : (k + 3) * 128]
+            parts[2 * owner + k, :, pl.ds(0, tokens)] = picked[k * tall : (k + 1) * tall]
+            others[2 * owner + k] = picked[(k + 2) * tall : (k + 3) * tall]
 
     local[2].wait()
-    place(cot_mine[...], z)
+    place(0)
+    pass_on(0)
+    for d in (2, 6, 1, 7):
+        if d in (1, 7):
+            z_wait(d)
+        place(d)
+    landed(2, 0, 0)
+    landed(2, 0, 1)
+    forward(2, 0, 2)
+    forward(2, 0, 3)
     pass_on(-1)
+    for d in (3, 5):
+        z_wait(d)
+        place(d)
+    z_wait(4, 0)
+    z_wait(4, 1)
+    place(4)
+    swap_parts = remote(others, parts.at[:, :, theirs], core_send.at[1], core_recv.at[1], twin)
+    swap_parts.start()
     pass_on(1)
-
-    def place_from(d, carry):
-        remote(cot_all.at[d], cot_all.at[d], z_send.at[d], z_recv.at[d], twin).wait_recv()
-        place(cot_all[d], lax.rem(z + 7 - d, 8))
-        return carry
-
-    lax.fori_loop(0, 7, place_from, 0)
-    swap_parts = remote(others, parts.at[:, theirs], core_send.at[1], core_recv.at[1], twin)
-    swap_parts.start()
-    pass_on(2)
     swap_hidden.wait()
     swap_parts.wait_recv()
 
     def product(p):
-        return lax.dot_general(
-            parts[p], hidden[...], (((0,), (0,)), ((), ())), preferred_element_type=F32
-        )[:rows]
+        return jnp.dot(parts[p], hidden[...], preferred_element_type=F32)[:rows]
 
     def offset(n):
         return jnp.where(n < 2, n + 2, 3 - n)
@@ -234,29 +261,9 @@
 
     lax.fori_loop(0, 4, start_far, 0)
 
-    def rest(t, carry):
-        n, m = t // 3, lax.rem(t, 3)
-        partial[n, m] = product(block(offset(n), jnp.where(m == 0, 1, jnp.where(m == 1, 3, 0))))
-        return carry
-
-    lax.fori_loop(0, 12, rest, 0)
-
-    for i in (0, -1, 1, 2):
-        landed(i, 2, 0)
-        landed(i, 2, 1)
-    local[3].wait()
-    acc[...] = jnp.zeros_like(acc)
-
-    def accumulate(p, carry):
-        acc[...] += jnp.dot(parts[p][:, :rows], weights_all[p], preferred_element_type=F32)
-        return carry
-
-    lax.fori_loop(0, 16, accumulate, 0)
-    swap_acc = remote(acc.at[theirs], acc_in, core_send.at[2], core_recv.at[2], twin)
-    swap_acc.start()
-
     def pass_full(n, carry):
         for side, (part, way) in enumerate(((lo, 1), (hi, -1))):
+            partial[n, side] = product(block(offset(n), (1, 3)[side]))
             remote(half_in.at[n, part], half_in.at[n, part], a_send.at[n, side], h_recv.at[n, side], twin).wait_recv()
             first = partial[n, side, lo]
             second = partial[n, side, hi]
@@ -271,21 +278,44 @@
         return carry
 
     lax.fori_loop(0, 4, pass_full, 0)
-
-    swap_acc.wait_recv()
+    pass_on(2)
+
+    def rest(n, carry):
+        partial[n, 2] = product(block(offset(n), 0))
+        return carry
+
+    lax.fori_loop(0, 4, rest, 0)
+
+    for i in (0, -1, 1, 2):
+        landed(i, 2, 0)
+        landed(i, 2, 1)
+    local[3].wait()
+    acc[...] = jnp.zeros_like(acc)
+
+    def accumulate(p, carry):
+        acc[...] += lax.dot_general(
+            parts[p, pl.ds(0, rows)], weights_all[p], (((0,), (0,)), ((), ())), preferred_element_type=F32
+        )
+        return carry
+
+    lax.fori_loop(0, 16, accumulate, 0)
+    swap_acc = remote(acc.at[theirs], acc_in, core_send.at[2], core_recv.at[2], twin)
+    swap_acc.start()
+
+    def finish(start, size):
+        here = pl.ds(start, size)
+        total = (acc[mine, here] + acc_in[:, here]).T
+        up_out[here] = (total * act[here]).astype(BF16)
+        gate_out[here] = (total * up_slope[here]).astype(BF16)
+
     outs = []
 
-    def finish(n, carry):
-        at_rows = pl.ds(pl.multiple_of(n * 16, 16), 16)
-        total = acc[at_rows] + acc_in[at_rows]
-        up_out[at_rows] = (total * act[at_rows]).astype(BF16)
-        gate_out[at_rows] = (total * up_slope[at_rows]).astype(BF16)
-        return carry
-
-    lax.fori_loop(0, tokens // 16, finish, 0)
-    for n, (src, dst) in enumerate(((gate_out, d_gate), (up_out, d_up))):
-        outs.append(pltpu.make_async_copy(src, dst, out_sem.at[n]))
-        outs[-1].start()
+    def write_tokens():
+        swap_acc.wait_recv()
+        over_units(finish)
+        for n, (src, dst) in enumerate(((gate_out, d_gate), (up_out, d_up))):
+            outs.append(pltpu.make_async_copy(src, dst, out_sem.at[n]))
+            outs[-1].start()
 
     def ring_sum(n):
         for side in range(2):
@@ -299,6 +329,7 @@
     ]
     for copy in far:
         copy.start()
+    write_tokens()
     full1 = []
     for n, side in ((1, 1), (2, 0)):
         down_out[...] = ring_sum(n)
@@ -335,9 +366,8 @@
     tokens, ff = gate_pre.shape
     rows = down_weight.shape[0]
     width = grad_out.shape[1]
-    low = 40
+    low, tall = 40, 96
     hbm = pl.BlockSpec(memory_space=pl.ANY)
-    vmem = pl.BlockSpec(memory_space=pltpu.VMEM)
     smem = pl.BlockSpec(memory_space=pltpu.SMEM)
     dma = pltpu.SemaphoreType.DMA
 
@@ -346,19 +376,21 @@
 
     scratch = [
         pltpu.VMEM((16, rows, ff), BF16),
-        pltpu.VMEM((7, tokens, width), BF16),
-        pltpu.VMEM((tokens, width), BF16),
+        pltpu.VMEM((8, width, tokens), BF16),
         pltpu.VMEM((2 * tokens, ff), BF16),
-        pltpu.VMEM((tokens, ff), BF16),
-        pltpu.VMEM((tokens, ff), BF16),
-        pltpu.VMEM((tokens, ff), F32),
-        pltpu.VMEM((tokens, ff), F32),
-        pltpu.VMEM((16, 2 * tokens, 128), BF16),
-        pltpu.VMEM((16, tokens, 128), BF16),
+        pltpu.VMEM((ff, tokens), BF16),
+        pltpu.VMEM((ff, tokens), BF16),
+        pltpu.VMEM((ff, tokens), F32),
+        pltpu.VMEM((ff, tokens), F32),
+        pltpu.VMEM((16, tall, 2 * tokens), BF16),
+        pltpu.VMEM((16, tall, tokens), BF16),
         pltpu.VMEM((2 * tokens, ff), F32),
         pltpu.VMEM((tokens, ff), F32),
         pltpu.VMEM((3, 16, tokens), F32),
         pltpu.VMEM((7, 16, tokens), F32),
+        pltpu.VMEM((1, tokens), F32),
+        pltpu.VMEM((1, tokens), F32),
+        pltpu.VMEM((1, tokens), jnp.int32),
         pltpu.VMEM((4, 3, rows, ff), F32),
         pltpu.VMEM((4, rows, ff), BF16),
         pltpu.VMEM((4, 2, rows, ff), BF16),
@@ -368,28 +400,29 @@
         pltpu.VMEM((2, rows, ff), BF16),
         pltpu.VMEM((rows, ff), BF16),
         pltpu.VMEM((2, rows, ff), BF16),
-        pltpu.VMEM((tokens, ff), BF16),
-        pltpu.VMEM((tokens, ff), BF16),
+        pltpu.VMEM((ff, tokens), BF16),
+        pltpu.VMEM((ff, tokens), BF16),
         pltpu.VMEM((rows, ff), F32),
-        dma((4,)), dma((3,)), dma((7,)), dma((7,)), dma((7,)), dma((7,)), dma((20,)), dma((20,)), dma((3,)), dma((3,)),
+        dma((7,)), dma((3,)), dma((7,)), dma((7,)), dma((8,)), dma((8,)), dma((20,)), dma((20,)), dma((3,)), dma((3,)),
         dma((4, 2)), dma((4, 2)), dma((4, 2)), dma((4, 2)), dma((2,)), dma((2,)), dma((2,)), dma((2,)),
     ]
-    return pl.pallas_call(
+    d_gate, d_up, d_down = pl.pallas_call(
         functools.partial(kernel, rows, low),
         out_shape=(
-            jax.ShapeDtypeStruct((tokens, ff), BF16),
-            jax.ShapeDtypeStruct((tokens, ff), BF16),
+            jax.ShapeDtypeStruct((ff, tokens), BF16),
+            jax.ShapeDtypeStruct((ff, tokens), BF16),
             jax.ShapeDtypeStruct((rows, ff), F32),
         ),
-        in_specs=[hbm, hbm, hbm, hbm, vmem, vmem, vmem, smem, smem],
+        in_specs=[hbm, hbm, hbm, hbm, hbm, hbm, hbm, smem, smem],
         out_specs=(hbm, hbm, hbm),
         scratch_shapes=scratch,
         compiler_params=pltpu.CompilerParams(
             collective_id=0, has_side_effects=True, vmem_limit_bytes=60 * 1024 * 1024
         ),
     )(
-        down_weight, grad_out, gate_pre, up_pre, line(new_logp), line(behav_logp), line(token_lag), lengths, versions
+        down_weight, grad_out.T, gate_pre.T, up_pre.T, line(new_logp), line(behav_logp), line(token_lag), lengths, versions
     )
+    return d_gate.T, d_up.T, d_down
 
 
 def solution(mesh):

time: 72.1 us -> 73.7 us (1.022); the launches traced: 71.9 us -> 72.6 us
  Pallas kernels: 61.7 us -> 66.9 us
  local copies, waits for them, and re-layouts: 8.24 us -> 3.72 us
    pallas_call x1, Pallas kernels: 61.7 us -> 66.9 us  [local(): pl.pallas_call(functools.partial(kernel, rows, low), out_shape=(jax.Shape...]
    pallas_call x2 -> x0, local copies, waits for them, and re-layouts: 2.85 us -> none  [local(): pl.pallas_call(functools.partial(kernel, rows, low), out_shape=(jax.Shape...]
    unnamed x10 -> x7, local copies, waits for them, and re-layouts: 5.39 us -> 3.72 us
where the time goes in v2:
time: 73.7 us; the launch traced here: 72.6 us
  Pallas kernels  66.9 us (91%)
  local copies, waits for them, and re-layouts  3.72 us (5%)
  between operations  1.94 us (3%)
    pallas_call x1, Pallas kernels, local(): pl.pallas_call(functools.partial(kernel, rows, low), out_shape=(jax.Shape...  66.9 us
    unnamed x7, local copies, waits for them, and re-layouts  3.72 us

profile of v2, /device:TPU:1, one launch (start us, length us, event | category | flops | bytes accessed | tf_op | source)
XLA Modules:
  0.0 72.6 jit_solution(18396157158691252353)
XLA Ops:
  1.9 66.9 %shard_map.112 = (bf16[1344,128]{1,0:T(8,128)(2,1)}, bf16[1344,128]{1,0:T(8,128)(2,1)}, f32[84,1344]{1,0:T(8,128)}) custom-call(bf16[84,1344]{1,0:T(8,128)(2,1)} %weight.1, bf16[336,128]{1,0:T(8,128)(2,1)} %bitcast.12, bf16[1344,128]{1,0:T(8,128)(2,1)} %bitcast.8, bf16[1344,128]{1,0:T(8,128)(2,1)} %bitcast.9, f32[1,128]{1,0:T(1,128)} %bitcast.13, ...), custom_call_target="tpu_custom_call" | custom-call | tf_op jit(solution)/shard_map/pallas_call | solution.py:409
  68.8 0.0 copy-start.1
  68.8 1.8 %copy.17 = bf16[128,1344]{0,1:T(8,128)(2,1)} copy(bf16[128,1344]{0,1:T(8,128)(2,1)} %bitcast.11) | data formatting | bytes 688128
  70.6 0.0 copy-done.1
  70.6 0.0 copy-start
  70.6 0.7 %copy.18 = bf16[128,1344]{0,1:T(8,128)(2,1)} copy(bf16[128,1344]{0,1:T(8,128)(2,1)S(1)} %bitcast.10) | data formatting | bytes 688128
  71.4 0.4 copy-done
  71.8 0.8 %copy.19 = f32[84,1344]{1,0:T(8,128)} copy(f32[84,1344]{1,0:T(8,128)S(1)} %copy-done) | data formatting | bytes 903168
Async XLA Ops:
  68.8 1.8 %copy-start.1 = (bf16[1344,128]{1,0:T(8,128)(2,1)S(1)}, bf16[1344,128]{1,0:T(8,128)(2,1)}, u32[]{:S(2)}) copy-start(bf16[1344,128]{1,0:T(8,128)(2,1)} %get-tuple-element.7) | copy-start | bytes 1032196
  70.6 1.2 %copy-start = (f32[84,1344]{1,0:T(8,128)S(1)}, f32[84,1344]{1,0:T(8,128)}, u32[]{:S(2)}) copy-start(f32[84,1344]{1,0:T(8,128)} %get-tuple-element.14) | copy-start | bytes 1354756

commit v3 on v2

--- a/solution.py
+++ b/solution.py
@@ -20,11 +20,11 @@
 
 def kernel(
     rows, low, weight, cotangent, gate, up, new_logp, old_logp, lag, length, version,
-    d_gate, d_up, d_down,
+    gate_out, up_out, down_out,
     weights_all, cot_all, hidden, gate_v, up_v, act, up_slope, parts, others, acc, acc_in, hist_out, hist_in,
     new_v, old_v, lag_v,
-    partial, far_out, full_out, half_in, full_in, far_out1, full_out1, half_in1, full_in1, gate_out, up_out, down_out,
-    copy_sem, out_sem, hist_send, hist_recv, z_send, z_recv, ag_send, ag_recv, core_send, core_recv,
+    partial, far_out, full_out, half_in, full_in, far_out1, full_out1, half_in1, full_in1,
+    copy_sem, hist_send, hist_recv, z_send, z_recv, ag_send, ag_recv, core_send, core_recv,
     a_send, f_send, h_recv, f_recv, a1_send, f1_send, h1_recv, f1_recv,
 ):
     y, x, c, z = (lax.axis_index(name) for name in (*DP, "mp"))
@@ -84,6 +84,34 @@
     counts = jnp.broadcast_to(jnp.sum(match, axis=1, keepdims=True), (16, tokens))
     hist_out[0] = counts
 
+    local[0].wait()
+    local[1].wait()
+
+    def elementwise(start, size):
+        here = pl.ds(start, size)
+        v = gate_v[here].astype(F32)
+        u = up_v[here].astype(F32)
+        square = v * v
+        t = jnp.tanh(ROOT * (v + CUBIC * (square * v)))
+        half = 0.5 * (1.0 + t)
+        a = v * half
+        slope = half + (0.5 * v) * (1.0 - t * t) * (ROOT * (1.0 + (3.0 * CUBIC) * square))
+        act[here] = a
+        up_slope[here] = u * slope
+        hidden[pl.ds(0, tokens), here] = (a * u).T.astype(BF16)
+
+    def over_units(body, first, last):
+        def step(n, carry):
+            body(pl.multiple_of(n * 128, 128), 128)
+            return carry
+
+        lax.fori_loop(first, min(last, units // 128), step, 0)
+        if last > units // 128 and units % 128:
+            body(units // 128 * 128, units % 128)
+
+    chunks = pl.cdiv(units, 128)
+    early = 4
+    over_units(elementwise, 0, early)
     pl.semaphore_wait(barrier, len(peers))
 
     sent = []
@@ -123,7 +151,7 @@
             sem, part = halves[(i, j)] + half, slot.at[lo if half == 0 else hi]
         remote(part, part, ag_send.at[0], ag_recv.at[sem], twin).wait_recv()
 
-    for way in range(4):
+    for way in range(2):
         forward(0, 0, way, src=weight)
     width = cotangent.shape[0]
     front, back = pl.ds(0, width // 2), pl.ds(width // 2, width // 2)
@@ -136,32 +164,7 @@
     for n, (d, slot) in enumerate(((2, 2), (-2, 6), (1, 1), (-1, 7))):
         go(remote(cotangent, cot_all.at[slot], z_send.at[n], z_recv.at[slot - 1], z_peers[d]))
 
-    local[0].wait()
-    local[1].wait()
-
-    def elementwise(start, size):
-        here = pl.ds(start, size)
-        v = gate_v[here].astype(F32)
-        u = up_v[here].astype(F32)
-        square = v * v
-        t = jnp.tanh(ROOT * (v + CUBIC * (square * v)))
-        half = 0.5 * (1.0 + t)
-        a = v * half
-        slope = half + (0.5 * v) * (1.0 - t * t) * (ROOT * (1.0 + (3.0 * CUBIC) * square))
-        act[here] = a
-        up_slope[here] = u * slope
-        hidden[pl.ds(0, tokens), here] = (a * u).T.astype(BF16)
-
-    def over_units(body):
-        def step(n, carry):
-            body(pl.multiple_of(n * 128, 128), 128)
-            return carry
-
-        lax.fori_loop(0, units // 128, step, 0)
-        if units % 128:
-            body(units // 128 * 128, units % 128)
-
-    over_units(elementwise)
+    over_units(elementwise, early, chunks)
     mine, theirs = pl.ds(0, tokens), pl.ds(tokens, tokens)
     swap_hidden = remote(hidden.at[mine], hidden.at[theirs], core_send.at[0], core_recv.at[0], twin)
     swap_hidden.start()
@@ -175,6 +178,8 @@
     for d in range(3):
         go(remote(hist_out.at[1], hist_in.at[3 + d], hist_send.at[3 + d], hist_recv.at[3 + d], y_peers[d]))
 
+    for way in range(2, 4):
+        forward(0, 0, way, src=weight)
     z_wait(2)
     go(remote(cot_all.at[2], cot_all.at[3], z_send.at[4], z_recv.at[2], z_peers[1]))
     go(remote(cot_all.at[2, front], cot_all.at[4, front], z_send.at[5], z_recv.at[3], z_peers[2]))
@@ -225,16 +230,16 @@
 
     local[2].wait()
     place(0)
+    place(2)
+    place(6)
     pass_on(0)
-    for d in (2, 6, 1, 7):
-        if d in (1, 7):
-            z_wait(d)
+    for d in (1, 7):
+        z_wait(d)
         place(d)
     landed(2, 0, 0)
     landed(2, 0, 1)
     forward(2, 0, 2)
     forward(2, 0, 3)
-    pass_on(-1)
     for d in (3, 5):
         z_wait(d)
         place(d)
@@ -243,6 +248,7 @@
     place(4)
     swap_parts = remote(others, parts.at[:, :, theirs], core_send.at[1], core_recv.at[1], twin)
     swap_parts.start()
+    pass_on(-1)
     pass_on(1)
     swap_hidden.wait()
     swap_parts.wait_recv()
@@ -277,45 +283,35 @@
             remote(full_out.at[n, side], full_in.at[n, side], f_send.at[n, side], f_recv.at[n, side], device(0, way)).start()
         return carry
 
-    lax.fori_loop(0, 4, pass_full, 0)
-    pass_on(2)
-
     def rest(n, carry):
         partial[n, 2] = product(block(offset(n), 0))
         return carry
 
+    def accumulate(group, first=False):
+        total = None if first else acc[...]
+        for i, j in group:
+            p = block(i, j)
+            term = lax.dot_general(
+                parts[p, pl.ds(0, rows)], weights_all[p], (((0,), (0,)), ((), ())), preferred_element_type=F32
+            )
+            total = term if total is None else total + term
+        acc[...] = total
+
+    local[3].wait()
+    accumulate(((0, 0), (-1, 0), (1, 0), (2, 0)), first=True)
+    lax.fori_loop(0, 4, pass_full, 0)
+    pass_on(2)
+    accumulate(((0, -1), (0, 1), (-1, -1), (-1, 1)))
     lax.fori_loop(0, 4, rest, 0)
-
-    for i in (0, -1, 1, 2):
-        landed(i, 2, 0)
-        landed(i, 2, 1)
-    local[3].wait()
-    acc[...] = jnp.zeros_like(acc)
-
-    def accumulate(p, carry):
-        acc[...] += lax.dot_general(
-            parts[p, pl.ds(0, rows)], weights_all[p], (((0,), (0,)), ((), ())), preferred_element_type=F32
-        )
-        return carry
-
-    lax.fori_loop(0, 16, accumulate, 0)
-    swap_acc = remote(acc.at[theirs], acc_in, core_send.at[2], core_recv.at[2], twin)
-    swap_acc.start()
-
     def finish(start, size):
         here = pl.ds(start, size)
         total = (acc[mine, here] + acc_in[:, here]).T
         up_out[here] = (total * act[here]).astype(BF16)
         gate_out[here] = (total * up_slope[here]).astype(BF16)
 
-    outs = []
-
     def write_tokens():
         swap_acc.wait_recv()
-        over_units(finish)
-        for n, (src, dst) in enumerate(((gate_out, d_gate), (up_out, d_up))):
-            outs.append(pltpu.make_async_copy(src, dst, out_sem.at[n]))
-            outs[-1].start()
+        over_units(finish, 0, chunks)
 
     def ring_sum(n):
         for side in range(2):
@@ -329,7 +325,7 @@
     ]
     for copy in far:
         copy.start()
-    write_tokens()
+    accumulate(((1, -1), (1, 1), (2, -1), (2, 1)))
     full1 = []
     for n, side in ((1, 1), (2, 0)):
         down_out[...] = ring_sum(n)
@@ -341,12 +337,18 @@
             remote(full_out1.at[side], full_in1.at[side], f1_send.at[side], f1_recv.at[side], device(way, 0))
         )
         full1[-1].start()
+    last = (0, -1, 1, 2)
+    for i in last:
+        landed(i, 2, 0)
+        landed(i, 2, 1)
+    accumulate([(i, 2) for i in last])
+    swap_acc = remote(acc.at[theirs], acc_in, core_send.at[2], core_recv.at[2], twin)
+    swap_acc.start()
+    write_tokens()
     down_out[...] = ring_sum(3)
     for copy in full1:
         copy.wait_recv()
     down_out[...] += full_in1[0].astype(F32) + full_in1[1].astype(F32)
-    outs.append(pltpu.make_async_copy(down_out, d_down, out_sem.at[2]))
-    outs[-1].start()
 
     for copy in (*sent, *far, *full1, swap_parts, swap_acc):
         copy.wait_send()
@@ -358,7 +360,14 @@
         return carry
 
     lax.fori_loop(0, 4, drain, 0)
-    for copy in outs:
+
+
+def write_out(*refs):
+    sem = refs[-1]
+    copies = [pltpu.make_async_copy(refs[n], refs[3 + n], sem.at[n]) for n in range(3)]
+    for copy in copies:
+        copy.start()
+    for copy in copies:
         copy.wait()
 
 
@@ -400,21 +409,19 @@
         pltpu.VMEM((2, rows, ff), BF16),
         pltpu.VMEM((rows, ff), BF16),
         pltpu.VMEM((2, rows, ff), BF16),
-        pltpu.VMEM((ff, tokens), BF16),
-        pltpu.VMEM((ff, tokens), BF16),
-        pltpu.VMEM((rows, ff), F32),
-        dma((7,)), dma((3,)), dma((7,)), dma((7,)), dma((8,)), dma((8,)), dma((20,)), dma((20,)), dma((3,)), dma((3,)),
+        dma((7,)), dma((7,)), dma((7,)), dma((8,)), dma((8,)), dma((20,)), dma((20,)), dma((3,)), dma((3,)),
         dma((4, 2)), dma((4, 2)), dma((4, 2)), dma((4, 2)), dma((2,)), dma((2,)), dma((2,)), dma((2,)),
     ]
-    d_gate, d_up, d_down = pl.pallas_call(
+    outs = (
+        jax.ShapeDtypeStruct((ff, tokens), BF16),
+        jax.ShapeDtypeStruct((ff, tokens), BF16),
+        jax.ShapeDtypeStruct((rows, ff), F32),
+    )
+    values = pl.pallas_call(
         functools.partial(kernel, rows, low),
-        out_shape=(
-            jax.ShapeDtypeStruct((ff, tokens), BF16),
-            jax.ShapeDtypeStruct((ff, tokens), BF16),
-            jax.ShapeDtypeStruct((rows, ff), F32),
-        ),
+        out_shape=tuple(pltpu.VMEM(o.shape, o.dtype) for o in outs),
         in_specs=[hbm, hbm, hbm, hbm, hbm, hbm, hbm, smem, smem],
-        out_specs=(hbm, hbm, hbm),
+        out_specs=(pl.BlockSpec(memory_space=pltpu.VMEM),) * 3,
         scratch_shapes=scratch,
         compiler_params=pltpu.CompilerParams(
             collective_id=0, has_side_effects=True, vmem_limit_bytes=60 * 1024 * 1024
@@ -422,6 +429,13 @@
     )(
         down_weight, grad_out.T, gate_pre.T, up_pre.T, line(new_logp), line(behav_logp), line(token_lag), lengths, versions
     )
+    d_gate, d_up, d_down = pl.pallas_call(
+        write_out,
+        out_shape=outs,
+        in_specs=[pl.BlockSpec(memory_space=pltpu.VMEM)] * 3,
+        out_specs=(hbm, hbm, hbm),
+        scratch_shapes=[dma((3,))],
+    )(*(pltpu.with_memory_space_constraint(v, pltpu.VMEM) for v in values))
     return d_gate.T, d_up.T, d_down
 
 

time: 73.7 us -> 62.9 us (0.85); the launches traced: 72.6 us -> 62.8 us
  Pallas kernels: 66.9 us -> 60.9 us
  local copies, waits for them, and re-layouts: 3.72 us -> 0 us
    pallas_call x1 -> x2, Pallas kernels: 66.9 us -> 60.9 us  [the longest x1 59.8 us: local(): pl.pallas_call(functools.partial(kernel, rows, low), out_shape=tuple((plt...]
    unnamed x7 -> x0, local copies, waits for them, and re-layouts: 3.72 us -> none
where the time goes in v3:
time: 62.9 us; the launch traced here: 62.8 us
  Pallas kernels  60.9 us (97%)
  between operations  1.93 us (3%)
    pallas_call x1, Pallas kernels, local(): pl.pallas_call(functools.partial(kernel, rows, low), out_shape=tuple((plt...  59.8 us

profile of v3, /device:TPU:1, one launch (start us, length us, event | category | flops | bytes accessed | tf_op | source)
XLA Modules:
  0.0 62.8 jit_solution(11448246996492835816)
XLA Ops:
  1.9 59.8 %shard_map.112 = (bf16[1344,128]{1,0:T(8,128)(2,1)S(1)}, bf16[1344,128]{1,0:T(8,128)(2,1)S(1)}, f32[84,1344]{1,0:T(8,128)S(1)}) custom-call(bf16[84,1344]{1,0:T(8,128)(2,1)} %weight.1, bf16[336,128]{1,0:T(8,128)(2,1)} %bitcast.10, bf16[1344,128]{1,0:T(8,128)(2,1)} %bitcast.8, bf16[1344,128]{1,0:T(8,128)(2,1)} %bitcast.9, f32[1,128]{1,0:T(1,128)} %bitcast.11, ...), custom_call_target="tpu_custom_call" | custom-call | tf_op jit(solution)/shard_map/pallas_call | solution.py:420
  61.8 1.0 %shard_map.113 = (bf16[1344,128]{1,0:T(8,128)(2,1)}, bf16[1344,128]{1,0:T(8,128)(2,1)}, f32[84,1344]{1,0:T(8,128)}) custom-call(bf16[1344,128]{1,0:T(8,128)(2,1)S(1)} %get-tuple-element.9.refs_0_, bf16[1344,128]{1,0:T(8,128)(2,1)S(1)} %get-tuple-element.10.refs_1_, f32[84,1344]{1,0:T(8,128)S(1)} %get-tuple-element.11.refs_2_), custom_call_target="tpu_custom_call" | custom-call | tf_op jit(solution)/shard_map/pallas_call | solution.py:432

commit v4 on v3

v4 whole, which is shorter than its diff:
```python
import functools
import math

import jax
import jax.numpy as jnp
from jax import lax
from jax.experimental import pallas as pl
from jax.experimental.pallas import tpu as pltpu
from jax.sharding import Mesh
from jax.sharding import PartitionSpec as P

MAX_LAG = 5
DP = ("dp_0", "dp_1", "dp_2")
MESH = pl.DeviceIdType.MESH
F32, BF16 = jnp.float32, jnp.bfloat16
RATIO_CAP = 2.0
ROOT = math.sqrt(2.0 / math.pi)
CUBIC = 0.044715


def kernel(
    rows, low, weight, cotangent, gate, up, new_logp, old_logp, lag, length, version,
    gate_out, up_out, down_out,
    weights_all, cot_all, hidden, gate_v, up_v, act, up_slope, pool, others, far, acc, acc_in, sum_out, sum_in, hist_out, hist_in,
    new_v, old_v, lag_v, partial, a_out, b_out, c_out, d_out, e_out, a_in, b_in, c_in, d_in, e_in,
    copy_sem, hist_send, hist_recv, z_send, z_recv, ag_send, ag_recv, core_send, core_recv, swap_send, swap_recv,
    cross_send, cross_recv, far_send, far_recv, rs_send, rs_recv,
):
    y, x, c, z = (lax.axis_index(name) for name in (*DP, "mp"))
    tokens, units = hidden.shape[0] // 4, hidden.shape[1]
    lo, hi = pl.ds(0, low), pl.ds(low, rows - low)
    side, column = x // 2, lax.rem(x, 2)

    def block(i, j):
        return lax.rem(y + 4 + j, 4) * 2 + lax.rem(column + i, 2)

    twin = (y, x, 1 - c, z)
    beside = (y, x + 1 - 2 * column, c, z)
    across = (y, 3 - x, c, z)
    ahead, behind = (lax.rem(y + 1, 4), x, c, z), (lax.rem(y + 3, 4), x, c, z)
    z_peers = {d: (y, x, c, lax.rem(z + 8 + d, 8)) for d in (-2, 2, -1, 1)}
    x_peers = [(y, lax.rem(x + d, 4), c, z) for d in range(1, 4)]
    y_peers = [(lax.rem(y + d, 4), x, c, z) for d in range(1, 4)]
    peers = [twin, *z_peers.values(), *x_peers, *y_peers]

    def remote(src, dst, send, recv, to):
        return pltpu.make_async_remote_copy(
            src_ref=src, dst_ref=dst, send_sem=send, recv_sem=recv, device_id=to, device_id_type=MESH
        )

    barrier = pltpu.get_barrier_semaphore()
    for peer in peers:
        pl.semaphore_signal(barrier, inc=1, device_id=peer, device_id_type=MESH)

    own = block(0, 0)
    local = [
        pltpu.make_async_copy(gate, gate_v, copy_sem.at[0]),
        pltpu.make_async_copy(up, up_v, copy_sem.at[1]),
        pltpu.make_async_copy(cotangent, cot_all.at[0], copy_sem.at[2]),
        pltpu.make_async_copy(weight, weights_all.at[own], copy_sem.at[3]),
    ]
    small = [
        pltpu.make_async_copy(src, dst, copy_sem.at[4 + n])
        for n, (src, dst) in enumerate(((lag, lag_v), (new_logp, new_v), (old_logp, old_v)))
    ]
    for copy in (*small, *local):
        copy.start()
    for copy in small:
        copy.wait()

    bins = lax.broadcasted_iota(jnp.int32, (16, tokens), 0)
    position = lax.broadcasted_iota(jnp.int32, (1, tokens), 1)
    live = position < length[0]
    token_version = lag_v[...] + version[0]
    match = jnp.where((token_version == bins) & live, 1.0, 0.0)
    counts = jnp.broadcast_to(jnp.sum(match, axis=1, keepdims=True), (16, tokens))
    hist_out[0] = counts

    local[0].wait()
    local[1].wait()

    def elementwise(start, size):
        here = pl.ds(start, size)
        v = gate_v[here].astype(F32)
        u = up_v[here].astype(F32)
        square = v * v
        t = jnp.tanh(ROOT * (v + CUBIC * (square * v)))
        half = 0.5 * (1.0 + t)
        a = v * half
        slope = half + (0.5 * v) * (1.0 - t * t) * (ROOT * (1.0 + (3.0 * CUBIC) * square))
        act[here] = a
        up_slope[here] = u * slope
        hidden[pl.ds(0, tokens), here] = (a * u).T.astype(BF16)

    def over_units(body, first, last):
        def step(n, carry):
            body(pl.multiple_of(n * 128, 128), 128)
            return carry

        lax.fori_loop(first, min(last, units // 128), step, 0)
        if last > units // 128 and units % 128:
            body(units // 128 * 128, units % 128)

    chunks = pl.cdiv(units, 128)
    early = 4
    over_units(elementwise, 0, early)
    pl.semaphore_wait(barrier, len(peers))

    sent = []

    def go(copy):
        copy.start()
        sent.append(copy)

    for d in range(3):
        go(remote(hist_out.at[0], hist_in.at[d], hist_send.at[d], hist_recv.at[d], x_peers[d]))

    slots = {(1, 0): 0, (0, -1): 1, (0, 1): 2, (1, -1): 3, (1, 1): 4, (0, 2): 5, (1, 2): 7}

    def spread(i, j, to, as_i, as_j, half=0, part=None, src=None):
        view = weights_all.at[block(i, j)]
        view = view if part is None else view.at[part]
        sem = slots[(as_i, as_j)] + half
        go(remote(view if src is None else src, view, ag_send.at[sem], ag_recv.at[sem], to))

    def landed(i, j, half=0, part=None):
        view = weights_all.at[block(i, j)]
        view = view if part is None else view.at[part]
        sem = slots[(i, j)] + half
        remote(view, view, ag_send.at[sem], ag_recv.at[sem], twin).wait_recv()

    width = cotangent.shape[0]
    front, back = pl.ds(0, width // 2), pl.ds(width // 2, width // 2)

    def z_wait(d, half=None):
        part = cot_all.at[d] if half is None else cot_all.at[d, (front, back)[half]]
        sem = d - 1 if half is None else (3, 7)[half]
        remote(part, part, z_send.at[0], z_recv.at[sem], twin).wait_recv()

    for n, (d, slot) in enumerate(((2, 2), (-2, 6), (1, 1), (-1, 7))):
        go(remote(cotangent, cot_all.at[slot], z_send.at[n], z_recv.at[slot - 1], z_peers[d]))
    spread(0, 0, beside, 1, 0, src=weight)
    spread(0, 0, ahead, 0, -1, src=weight)
    spread(0, 0, behind, 0, 1, src=weight)

    over_units(elementwise, early, chunks)
    quarter = [pl.ds(n * tokens, tokens) for n in range(4)]
    crossing = [
        remote(hidden.at[quarter[0]], hidden.at[quarter[2]], core_send.at[0], core_recv.at[0], across),
        remote(hidden.at[quarter[0]], hidden.at[quarter[1]], core_send.at[1], core_recv.at[1], twin),
        remote(hidden.at[quarter[2]], hidden.at[quarter[3]], core_send.at[2], core_recv.at[2], twin),
    ]
    crossing[0].start()
    crossing[1].start()

    def received(n):
        remote(hist_in.at[n], hist_in.at[n], hist_send.at[n], hist_recv.at[n], twin).wait_recv()
        return hist_in[n]

    counts = counts + received(0) + received(1) + received(2)
    hist_out[1] = counts
    for d in range(3):
        go(remote(hist_out.at[1], hist_in.at[3 + d], hist_send.at[3 + d], hist_recv.at[3 + d], y_peers[d]))

    z_wait(2)
    go(remote(cot_all.at[2], cot_all.at[3], z_send.at[4], z_recv.at[2], z_peers[1]))
    go(remote(cot_all.at[2, front], cot_all.at[4, front], z_send.at[5], z_recv.at[3], z_peers[2]))
    z_wait(6)
    go(remote(cot_all.at[6], cot_all.at[5], z_send.at[6], z_recv.at[4], z_peers[-1]))
    go(remote(cot_all.at[6, back], cot_all.at[4, back], z_send.at[7], z_recv.at[7], z_peers[-2]))

    counts = counts + received(3) + received(4) + received(5)
    hist_out[2] = counts
    go(remote(hist_out.at[2], hist_in.at[6], hist_send.at[6], hist_recv.at[6], twin))

    landed(1, 0)
    spread(1, 0, ahead, 1, -1)
    spread(1, 0, behind, 1, 1)
    landed(0, -1)
    spread(0, -1, ahead, 0, 2, 0, lo)
    landed(0, 1)
    spread(0, 1, behind, 0, 2, 1, hi)

    counts = counts + received(6)
    current = jnp.max(jnp.where(counts > 0, bins, -1), axis=0, keepdims=True)
    oldest = current - MAX_LAG
    valid_count = jnp.sum(jnp.where(bins >= oldest, counts, 0.0), axis=0, keepdims=True)
    valid = live & (token_version >= oldest)
    ratio = jnp.minimum(jnp.exp(new_v[...] - old_v[...]), RATIO_CAP)
    token_weight = jnp.where(valid, ratio, 0.0) * (32.0 / valid_count)

    tall = pool.shape[2]
    line = lax.broadcasted_iota(jnp.int32, (4 * tall, width), 0)
    source = lax.broadcasted_iota(jnp.int32, (4 * tall, width), 1)
    group = (line >= tall).astype(jnp.int32) + (line >= 2 * tall).astype(jnp.int32) + (line >= 3 * tall).astype(jnp.int32)
    row = line - tall * group
    parity = jnp.where(group < 2, c, 1 - c)
    wanted = rows * (2 * (group & 1) + parity) + row
    select = jnp.where((source == wanted) & (row < rows), 1.0, 0.0).astype(BF16)

    outgoing = lax.rem(z + side + 1, 2)

    def where(d):
        owner = lax.rem(z + 8 - d, 8)
        return lax.rem(owner, 2), owner // 2

    def swap(d):
        of, pair = where(d)
        pairs = pl.ds(pair * 2, 2)
        return remote(
            others.at[of, pairs], pool.at[of, pairs, :, pl.ds(tokens, tokens)], swap_send.at[d], swap_recv.at[d], twin
        )

    def place(d):
        of, pair = where(d)
        scaled = (token_weight * cot_all[d].astype(F32)).astype(BF16)
        picked = jnp.dot(select, scaled, preferred_element_type=F32)
        for k in range(2):
            pool[of, 2 * pair + k, :, pl.ds(0, tokens)] = picked[k * tall : (k + 1) * tall].astype(BF16)
            others[of, 2 * pair + k] = picked[(k + 2) * tall : (k + 3) * tall].astype(BF16)
        swap(d).start()

    def hand(pair):
        pairs = pl.ds(pair * 2, 2)
        return remote(pool.at[1 - side, pairs], far.at[pairs], far_send.at[pair], far_recv.at[pair], across)

    def export(d):
        swap(d).wait_recv()

        @pl.when(outgoing == d % 2)
        def _():
            hand(where(d)[1]).start()

    local[2].wait()
    for d in (0, 2, 6):
        place(d)
    for d in (1, 7):
        z_wait(d)
        place(d)
    for d in (0, 2, 6, 1, 7):
        export(d)
    landed(0, 2, 0, lo)
    landed(0, 2, 1, hi)
    spread(0, 2, beside, 1, 2)
    for d in (3, 5):
        z_wait(d)
        place(d)
    z_wait(4, 0)
    z_wait(4, 1)
    place(4)
    for d in (3, 5, 4):
        export(d)
    crossing[0].wait_recv()
    crossing[2].start()
    local[3].wait()
    landed(1, -1)
    landed(1, 1)
    landed(1, 2)

    near_rows, far_rows = pl.ds(0, 2 * tokens), pl.ds(2 * tokens, 2 * tokens)

    def accumulate(group, first):
        for source, here in ((pool.at[side], near_rows), (far, far_rows)):
            total = None if first else acc[here]
            for i, j in group:
                p = block(i, j)
                term = lax.dot_general(
                    source[p, pl.ds(0, rows)], weights_all[p], (((0,), (0,)), ((), ())), preferred_element_type=F32
                )
                total = term if total is None else total + term
            acc[here] = total

    crossing[1].wait_recv()
    for pair in range(4):
        hand(pair).wait_recv()
    crossing[2].wait_recv()

    targets = ((1, 2), (1, 1), (1, -1), (0, 2), (1, 0), (0, 1), (0, -1), (0, 0))

    def product(n, i, j):
        p = lax.rem(y + 4 + j, 4) * 2 + lax.rem(column + i, 2)
        near = jnp.dot(pool[side, p], hidden[near_rows], preferred_element_type=F32)
        partial[n] = (near + jnp.dot(far[p], hidden[far_rows], preferred_element_type=F32))[:rows]

    def shift(n):
        i = jnp.where((n < 3) | (n == 4), 1, 0)
        j = jnp.where((n == 0) | (n == 3), 2, jnp.where((n == 1) | (n == 5), 1, jnp.where((n == 2) | (n == 6), 3, 0)))
        return i, j

    def products(first, last):
        def step(n, carry):
            product(n, *shift(n))
            return carry

        lax.fori_loop(first, last, step, 0)

    sums = {
        "a": (a_out, a_in, 0, beside),
        "b0": (b_out.at[0], b_in.at[0], 1, ahead),
        "b1": (b_out.at[1], b_in.at[1], 2, behind),
        "c0": (c_out.at[lo], c_in.at[lo], 3, ahead),
        "c1": (c_out.at[hi], c_in.at[hi], 4, behind),
        "d": (d_out, d_in, 5, beside),
        "e0": (e_out.at[0], e_in.at[0], 6, ahead),
        "e1": (e_out.at[1], e_in.at[1], 7, behind),
    }
    sums = {key: remote(src, dst, rs_send.at[n], rs_recv.at[n], to) for key, (src, dst, n, to) in sums.items()}

    products(0, 3)
    a_out[...] = partial[0].astype(BF16)
    sums["a"].start()
    b_out[0] = partial[1].astype(BF16)
    sums["b0"].start()
    b_out[1] = partial[2].astype(BF16)
    sums["b1"].start()
    accumulate(((0, 0), (1, 0), (0, -1), (0, 1)), True)
    accumulate(((1, -1), (1, 1), (0, 2), (1, 2)), False)
    swaps = [
        remote(acc.at[quarter[2 * n + 1]], acc_in.at[n], cross_send.at[n], cross_recv.at[n], twin) for n in range(2)
    ]
    swaps[1].start()
    swaps[0].start()
    products(3, 8)
    sums["a"].wait_recv()
    c_out[...] = (partial[3] + a_in[...].astype(F32)).astype(BF16)
    sums["c0"].start()
    sums["c1"].start()
    swaps[1].wait_recv()
    sum_out[...] = (acc[quarter[2]] + acc_in[1]).astype(BF16)
    sum_cross = remote(sum_out, sum_in, cross_send.at[2], cross_recv.at[2], across)
    sum_cross.start()
    sums["b0"].wait_recv()
    sums["b1"].wait_recv()
    d_out[...] = (partial[4] + b_in[0].astype(F32) + b_in[1].astype(F32)).astype(BF16)
    sums["d"].start()
    sums["c0"].wait_recv()
    partial[5, lo] += c_in[lo].astype(F32)
    e_out[0] = partial[5].astype(BF16)
    sums["e0"].start()
    sums["c1"].wait_recv()
    partial[6, hi] += c_in[hi].astype(F32)
    e_out[1] = partial[6].astype(BF16)
    sums["e1"].start()

    def finish(start, size):
        here = pl.ds(start, size)
        total = (acc[quarter[0], here] + acc_in[0, :, here] + sum_in[:, here].astype(F32)).T
        up_out[here] = (total * act[here]).astype(BF16)
        gate_out[here] = (total * up_slope[here]).astype(BF16)

    swaps[0].wait_recv()
    sum_cross.wait_recv()
    over_units(finish, 0, chunks)
    sums["d"].wait_recv()
    down_out[...] = partial[7] + d_in[...].astype(F32)
    sums["e0"].wait_recv()
    sums["e1"].wait_recv()
    down_out[...] += e_in[0].astype(F32) + e_in[1].astype(F32)

    for copy in (*sent, *crossing, *swaps, sum_cross, *sums.values()):
        copy.wait_send()
    for d in range(8):
        swap(d).wait_send()
    for pair in range(4):
        hand(pair).wait_send()


def write_out(*refs):
    sem = refs[-1]
    copies = [pltpu.make_async_copy(refs[n], refs[3 + n], sem.at[n]) for n in range(3)]
    for copy in copies:
        copy.start()
    for copy in copies:
        copy.wait()


def local(grad_out, gate_pre, up_pre, down_weight, new_logp, behav_logp, lengths, versions, token_lag):
    tokens, ff = gate_pre.shape
    rows = down_weight.shape[0]
    width = grad_out.shape[1]
    low, tall = 40, 88
    hbm = pl.BlockSpec(memory_space=pl.ANY)
    smem = pl.BlockSpec(memory_space=pltpu.SMEM)
    dma = pltpu.SemaphoreType.DMA

    def line(values):
        return values.reshape(1, tokens)

    scratch = [
        pltpu.VMEM((8, rows, ff), BF16),
        pltpu.VMEM((8, width, tokens), BF16),
        pltpu.VMEM((4 * tokens, ff), BF16),
        pltpu.VMEM((ff, tokens), BF16),
        pltpu.VMEM((ff, tokens), BF16),
        pltpu.VMEM((ff, tokens), F32),
        pltpu.VMEM((ff, tokens), F32),
        pltpu.VMEM((2, 8, tall, 2 * tokens), BF16),
        pltpu.VMEM((2, 8, tall, tokens), BF16),
        pltpu.VMEM((8, tall, 2 * tokens), BF16),
        pltpu.VMEM((4 * tokens, ff), F32),
        pltpu.VMEM((2, tokens, ff), F32),
        pltpu.VMEM((tokens, ff), BF16),
        pltpu.VMEM((tokens, ff), BF16),
        pltpu.VMEM((3, 16, tokens), F32),
        pltpu.VMEM((7, 16, tokens), F32),
        pltpu.VMEM((1, tokens), F32),
        pltpu.VMEM((1, tokens), F32),
        pltpu.VMEM((1, tokens), jnp.int32),
        pltpu.VMEM((8, rows, ff), F32),
        *(
            pltpu.VMEM((*lead, rows, ff), BF16)
            for lead in ((), (2,), (), (), (2,), (), (2,), (), (), (2,))
        ),
        dma((7,)), dma((7,)), dma((7,)), dma((8,)), dma((8,)), dma((8,)), dma((8,)), dma((3,)), dma((3,)), dma((8,)), dma((8,)),
        dma((3,)), dma((3,)), dma((4,)), dma((4,)), dma((8,)), dma((8,)),
    ]
    outs = (
        jax.ShapeDtypeStruct((ff, tokens), BF16),
        jax.ShapeDtypeStruct((ff, tokens), BF16),
        jax.ShapeDtypeStruct((rows, ff), F32),
    )
    values = pl.pallas_call(
        functools.partial(kernel, rows, low),
        out_shape=tuple(pltpu.VMEM(o.shape, o.dtype) for o in outs),
        in_specs=[hbm, hbm, hbm, hbm, hbm, hbm, hbm, smem, smem],
        out_specs=(pl.BlockSpec(memory_space=pltpu.VMEM),) * 3,
        scratch_shapes=scratch,
        compiler_params=pltpu.CompilerParams(
            collective_id=0, has_side_effects=True, vmem_limit_bytes=60 * 1024 * 1024
        ),
    )(
        down_weight, grad_out.T, gate_pre.T, up_pre.T, line(new_logp), line(behav_logp), line(token_lag), lengths, versions
    )
    d_gate, d_up, d_down = pl.pallas_call(
        write_out,
        out_shape=outs,
        in_specs=[pl.BlockSpec(memory_space=pltpu.VMEM)] * 3,
        out_specs=(hbm, hbm, hbm),
        scratch_shapes=[dma((3,))],
    )(*(pltpu.with_memory_space_constraint(v, pltpu.VMEM) for v in values))
    return d_gate.T, d_up.T, d_down


def solution(mesh):
    split = Mesh(mesh.devices.reshape(4, 4, 2, mesh.shape["mp"]), (*DP, "mp"))
    placed = (P(DP, "mp"), P(DP, "mp"), P(DP, "mp"), P(DP, "mp"), P(DP), P(DP), P(DP), P(DP), P(DP))
    return jax.shard_map(
        local,
        mesh=split,
        in_specs=placed,
        out_specs=(P(DP, "mp"), P(DP, "mp"), P(DP, "mp")),
        check_vma=False,
    )
```

time: 62.9 us -> 55.8 us (0.89)
  Pallas kernels: 60.9 us -> 53.8 us
    pallas_call x1, Pallas kernels: 59.8 us -> 52.7 us  [local(): pl.pallas_call(functools.partial(kernel, rows, low), out_shape=tuple((plt...]
where the time goes in v4:
time: 55.8 us; the launch traced here: 55.7 us
  Pallas kernels  53.8 us (96%)
  between operations  1.93 us (3%)
    pallas_call x1, Pallas kernels, local(): pl.pallas_call(functools.partial(kernel, rows, low), out_shape=tuple((plt...  52.7 us

profile of v4, /device:TPU:1, one launch (start us, length us, event | category | flops | bytes accessed | tf_op | source)
XLA Modules:
  0.0 55.7 jit_solution(2603837920030928315)
XLA Ops:
  1.9 52.7 %shard_map.112 = (bf16[1344,128]{1,0:T(8,128)(2,1)S(1)}, bf16[1344,128]{1,0:T(8,128)(2,1)S(1)}, f32[84,1344]{1,0:T(8,128)S(1)}) custom-call(bf16[84,1344]{1,0:T(8,128)(2,1)} %weight.1, bf16[336,128]{1,0:T(8,128)(2,1)} %bitcast.10, bf16[1344,128]{1,0:T(8,128)(2,1)} %bitcast.8, bf16[1344,128]{1,0:T(8,128)(2,1)} %bitcast.9, f32[1,128]{1,0:T(1,128)} %bitcast.11, ...), custom_call_target="tpu_custom_call" | custom-call | tf_op jit(solution)/shard_map/pallas_call | solution.py:422
  54.7 1.0 %shard_map.113 = (bf16[1344,128]{1,0:T(8,128)(2,1)}, bf16[1344,128]{1,0:T(8,128)(2,1)}, f32[84,1344]{1,0:T(8,128)}) custom-call(bf16[1344,128]{1,0:T(8,128)(2,1)S(1)} %get-tuple-element.9.refs_0_, bf16[1344,128]{1,0:T(8,128)(2,1)S(1)} %get-tuple-element.10.refs_1_, f32[84,1344]{1,0:T(8,128)S(1)} %get-tuple-element.11.refs_2_), custom_call_target="tpu_custom_call" | custom-call | tf_op jit(solution)/shard_map/pallas_call | solution.py:434

commit v5 on v4

--- a/solution.py
+++ b/solution.py
@@ -22,9 +22,9 @@
     rows, low, weight, cotangent, gate, up, new_logp, old_logp, lag, length, version,
     gate_out, up_out, down_out,
     weights_all, cot_all, hidden, gate_v, up_v, act, up_slope, pool, others, far, acc, acc_in, sum_out, sum_in, hist_out, hist_in,
-    new_v, old_v, lag_v, partial, a_out, b_out, c_out, d_out, e_out, a_in, b_in, c_in, d_in, e_in,
+    new_v, old_v, lag_v, select, w_out, w_in, partial, a_out, b_out, c_out, d_out, e_out, a_in, b_in, c_in, d_in, e_in,
     copy_sem, hist_send, hist_recv, z_send, z_recv, ag_send, ag_recv, core_send, core_recv, swap_send, swap_recv,
-    cross_send, cross_recv, far_send, far_recv, rs_send, rs_recv,
+    cross_send, cross_recv, far_send, far_recv, rs_send, rs_recv, w_send, w_recv,
 ):
     y, x, c, z = (lax.axis_index(name) for name in (*DP, "mp"))
     tokens, units = hidden.shape[0] // 4, hidden.shape[1]
@@ -101,6 +101,18 @@
         if last > units // 128 and units % 128:
             body(units // 128 * 128, units % 128)
 
+    width = cotangent.shape[0]
+    front, back = pl.ds(0, width // 2), pl.ds(width // 2, width // 2)
+
+    tall = pool.shape[2]
+    line = lax.broadcasted_iota(jnp.int32, (4 * tall, width), 0)
+    source = lax.broadcasted_iota(jnp.int32, (4 * tall, width), 1)
+    group = (line >= tall).astype(jnp.int32) + (line >= 2 * tall).astype(jnp.int32) + (line >= 3 * tall).astype(jnp.int32)
+    row = line - tall * group
+    parity = jnp.where(group < 2, c, 1 - c)
+    wanted = rows * (2 * (group & 1) + parity) + row
+    select[...] = jnp.where((source == wanted) & (row < rows), 1.0, 0.0).astype(BF16)
+
     chunks = pl.cdiv(units, 128)
     early = 4
     over_units(elementwise, 0, early)
@@ -129,9 +141,6 @@
         sem = slots[(i, j)] + half
         remote(view, view, ag_send.at[sem], ag_recv.at[sem], twin).wait_recv()
 
-    width = cotangent.shape[0]
-    front, back = pl.ds(0, width // 2), pl.ds(width // 2, width // 2)
-
     def z_wait(d, half=None):
         part = cot_all.at[d] if half is None else cot_all.at[d, (front, back)[half]]
         sem = d - 1 if half is None else (3, 7)[half]
@@ -143,15 +152,53 @@
     spread(0, 0, ahead, 0, -1, src=weight)
     spread(0, 0, behind, 0, 1, src=weight)
 
-    over_units(elementwise, early, chunks)
+    outgoing = lax.rem(z + side + 1, 2)
+
+    def where(d):
+        owner = lax.rem(z + 8 - d, 8)
+        return lax.rem(owner, 2), owner // 2
+
+    def swap(d):
+        of, pair = where(d)
+        pairs = pl.ds(pair * 2, 2)
+        return remote(
+            others.at[of, pairs], pool.at[of, pairs, :, pl.ds(tokens, tokens)], swap_send.at[d], swap_recv.at[d], twin
+        )
+
+    def place(d):
+        of, pair = where(d)
+        picked = jnp.dot(select[...], cot_all[d], preferred_element_type=F32)
+        for k in range(2):
+            pool[of, 2 * pair + k, :, pl.ds(0, tokens)] = picked[k * tall : (k + 1) * tall].astype(BF16)
+            others[of, 2 * pair + k] = picked[(k + 2) * tall : (k + 3) * tall].astype(BF16)
+        swap(d).start()
+
+    def hand(pair):
+        pairs = pl.ds(pair * 2, 2)
+        return remote(pool.at[1 - side, pairs], far.at[pairs], far_send.at[pair], far_recv.at[pair], across)
+
+    def export(d):
+        swap(d).wait_recv()
+
+        @pl.when(outgoing == d % 2)
+        def _():
+            hand(where(d)[1]).start()
+
     quarter = [pl.ds(n * tokens, tokens) for n in range(4)]
+    first, second = pl.ds(0, early * 128), pl.ds(early * 128, units - early * 128)
     crossing = [
-        remote(hidden.at[quarter[0]], hidden.at[quarter[2]], core_send.at[0], core_recv.at[0], across),
+        remote(hidden.at[quarter[0], first], hidden.at[quarter[2], first], core_send.at[0], core_recv.at[0], across),
+        remote(hidden.at[quarter[0], second], hidden.at[quarter[2], second], core_send.at[3], core_recv.at[3], across),
         remote(hidden.at[quarter[0]], hidden.at[quarter[1]], core_send.at[1], core_recv.at[1], twin),
         remote(hidden.at[quarter[2]], hidden.at[quarter[3]], core_send.at[2], core_recv.at[2], twin),
     ]
     crossing[0].start()
+    local[2].wait()
+    place(0)
+    over_units(elementwise, early, chunks)
     crossing[1].start()
+    crossing[2].start()
+    export(0)
 
     def received(n):
         remote(hist_in.at[n], hist_in.at[n], hist_send.at[n], hist_recv.at[n], twin).wait_recv()
@@ -169,18 +216,28 @@
     go(remote(cot_all.at[6], cot_all.at[5], z_send.at[6], z_recv.at[4], z_peers[-1]))
     go(remote(cot_all.at[6, back], cot_all.at[4, back], z_send.at[7], z_recv.at[7], z_peers[-2]))
 
-    counts = counts + received(3) + received(4) + received(5)
-    hist_out[2] = counts
-    go(remote(hist_out.at[2], hist_in.at[6], hist_send.at[6], hist_recv.at[6], twin))
-
-    landed(1, 0)
-    spread(1, 0, ahead, 1, -1)
-    spread(1, 0, behind, 1, 1)
     landed(0, -1)
     spread(0, -1, ahead, 0, 2, 0, lo)
     landed(0, 1)
     spread(0, 1, behind, 0, 2, 1, hi)
-
+    landed(1, 0)
+    spread(1, 0, ahead, 1, -1)
+    spread(1, 0, behind, 1, 1)
+    counts = counts + received(3) + received(4) + received(5)
+    hist_out[2] = counts
+    go(remote(hist_out.at[2], hist_in.at[6], hist_send.at[6], hist_recv.at[6], twin))
+
+
+    place(2)
+    place(6)
+    for d in (1, 7):
+        z_wait(d)
+        place(d)
+    for d in (2, 6, 1, 7):
+        export(d)
+    landed(0, 2, 0, lo)
+    landed(0, 2, 1, hi)
+    spread(0, 2, beside, 1, 2)
     counts = counts + received(6)
     current = jnp.max(jnp.where(counts > 0, bins, -1), axis=0, keepdims=True)
     oldest = current - MAX_LAG
@@ -189,74 +246,41 @@
     ratio = jnp.minimum(jnp.exp(new_v[...] - old_v[...]), RATIO_CAP)
     token_weight = jnp.where(valid, ratio, 0.0) * (32.0 / valid_count)
 
-    tall = pool.shape[2]
-    line = lax.broadcasted_iota(jnp.int32, (4 * tall, width), 0)
-    source = lax.broadcasted_iota(jnp.int32, (4 * tall, width), 1)
-    group = (line >= tall).astype(jnp.int32) + (line >= 2 * tall).astype(jnp.int32) + (line >= 3 * tall).astype(jnp.int32)
-    row = line - tall * group
-    parity = jnp.where(group < 2, c, 1 - c)
-    wanted = rows * (2 * (group & 1) + parity) + row
-    select = jnp.where((source == wanted) & (row < rows), 1.0, 0.0).astype(BF16)
-
-    outgoing = lax.rem(z + side + 1, 2)
-
-    def where(d):
-        owner = lax.rem(z + 8 - d, 8)
-        return lax.rem(owner, 2), owner // 2
-
-    def swap(d):
-        of, pair = where(d)
-        pairs = pl.ds(pair * 2, 2)
-        return remote(
-            others.at[of, pairs], pool.at[of, pairs, :, pl.ds(tokens, tokens)], swap_send.at[d], swap_recv.at[d], twin
-        )
-
-    def place(d):
-        of, pair = where(d)
-        scaled = (token_weight * cot_all[d].astype(F32)).astype(BF16)
-        picked = jnp.dot(select, scaled, preferred_element_type=F32)
-        for k in range(2):
-            pool[of, 2 * pair + k, :, pl.ds(0, tokens)] = picked[k * tall : (k + 1) * tall].astype(BF16)
-            others[of, 2 * pair + k] = picked[(k + 2) * tall : (k + 3) * tall].astype(BF16)
-        swap(d).start()
-
-    def hand(pair):
-        pairs = pl.ds(pair * 2, 2)
-        return remote(pool.at[1 - side, pairs], far.at[pairs], far_send.at[pair], far_recv.at[pair], across)
-
-    def export(d):
-        swap(d).wait_recv()
-
-        @pl.when(outgoing == d % 2)
-        def _():
-            hand(where(d)[1]).start()
-
-    local[2].wait()
-    for d in (0, 2, 6):
-        place(d)
-    for d in (1, 7):
-        z_wait(d)
-        place(d)
-    for d in (0, 2, 6, 1, 7):
-        export(d)
-    landed(0, 2, 0, lo)
-    landed(0, 2, 1, hi)
-    spread(0, 2, beside, 1, 2)
+    w_out[...] = jnp.broadcast_to(token_weight, w_out.shape)
+    weighing = [
+        remote(w_out, w_in.at[0], w_send.at[0], w_recv.at[0], twin),
+        remote(w_out, w_in.at[1], w_send.at[1], w_recv.at[1], across),
+        remote(w_in.at[1], w_in.at[2], w_send.at[2], w_recv.at[2], twin),
+    ]
+    weighing[0].start()
+    weighing[1].start()
     for d in (3, 5):
         z_wait(d)
         place(d)
+    for d in (3, 5):
+        export(d)
+    weighing[1].wait_recv()
+    weighing[2].start()
     z_wait(4, 0)
     z_wait(4, 1)
     place(4)
-    for d in (3, 5, 4):
-        export(d)
+    export(4)
     crossing[0].wait_recv()
-    crossing[2].start()
-    local[3].wait()
-    landed(1, -1)
-    landed(1, 1)
-    landed(1, 2)
-
+    crossing[1].wait_recv()
+    crossing[3].start()
+    weighing[0].wait_recv()
+    weighing[2].wait_recv()
+
+    def scale(view, left, right):
+        def step(n, carry):
+            for k, row in enumerate((left, right)):
+                here = pl.ds(k * tokens, tokens)
+                view[n, :, here] = (row * view[n, :, here].astype(F32)).astype(BF16)
+            return carry
+
+        lax.fori_loop(0, 8, step, 0)
+
+    scale(pool.at[side], token_weight, w_in[0, 0:1])
     near_rows, far_rows = pl.ds(0, 2 * tokens), pl.ds(2 * tokens, 2 * tokens)
 
     def accumulate(group, first):
@@ -270,12 +294,11 @@
                 total = term if total is None else total + term
             acc[here] = total
 
-    crossing[1].wait_recv()
+    crossing[2].wait_recv()
     for pair in range(4):
         hand(pair).wait_recv()
-    crossing[2].wait_recv()
-
-    targets = ((1, 2), (1, 1), (1, -1), (0, 2), (1, 0), (0, 1), (0, -1), (0, 0))
+    scale(far, w_in[1, 0:1], w_in[2, 0:1])
+    crossing[3].wait_recv()
 
     def product(n, i, j):
         p = lax.rem(y + 4 + j, 4) * 2 + lax.rem(column + i, 2)
@@ -283,8 +306,8 @@
         partial[n] = (near + jnp.dot(far[p], hidden[far_rows], preferred_element_type=F32))[:rows]
 
     def shift(n):
-        i = jnp.where((n < 3) | (n == 4), 1, 0)
-        j = jnp.where((n == 0) | (n == 3), 2, jnp.where((n == 1) | (n == 5), 1, jnp.where((n == 2) | (n == 6), 3, 0)))
+        i = jnp.where((n < 3) | (n == 6), 1, 0)
+        j = jnp.where((n == 0) | (n == 5), 2, jnp.where((n == 1) | (n == 3), 1, jnp.where((n == 2) | (n == 4), 3, 0)))
         return i, j
 
     def products(first, last):
@@ -301,8 +324,10 @@
         "c0": (c_out.at[lo], c_in.at[lo], 3, ahead),
         "c1": (c_out.at[hi], c_in.at[hi], 4, behind),
         "d": (d_out, d_in, 5, beside),
-        "e0": (e_out.at[0], e_in.at[0], 6, ahead),
-        "e1": (e_out.at[1], e_in.at[1], 7, behind),
+        "e0": (e_out.at[0, lo], e_in.at[0, lo], 6, ahead),
+        "e1": (e_out.at[1, hi], e_in.at[1, hi], 7, behind),
+        "f0": (e_out.at[0, hi], e_in.at[0, hi], 8, ahead),
+        "f1": (e_out.at[1, lo], e_in.at[1, lo], 9, behind),
     }
     sums = {key: remote(src, dst, rs_send.at[n], rs_recv.at[n], to) for key, (src, dst, n, to) in sums.items()}
 
@@ -313,33 +338,45 @@
     sums["b0"].start()
     b_out[1] = partial[2].astype(BF16)
     sums["b1"].start()
+    local[3].wait()
     accumulate(((0, 0), (1, 0), (0, -1), (0, 1)), True)
+    landed(1, -1)
+    landed(1, 1)
+    landed(1, 2)
     accumulate(((1, -1), (1, 1), (0, 2), (1, 2)), False)
     swaps = [
         remote(acc.at[quarter[2 * n + 1]], acc_in.at[n], cross_send.at[n], cross_recv.at[n], twin) for n in range(2)
     ]
     swaps[1].start()
     swaps[0].start()
-    products(3, 8)
+    products(3, 5)
+    e_out[0, hi] = partial[3, hi].astype(BF16)
+    sums["f0"].start()
+    e_out[1, lo] = partial[4, lo].astype(BF16)
+    sums["f1"].start()
+    swaps[1].wait_recv()
+    ff_parts = [pl.ds(0, 640), pl.ds(640, units - 640)]
+    cross = []
+    for n, part in enumerate(ff_parts):
+        sum_out[:, part] = (acc[quarter[2], part] + acc_in[1, :, part]).astype(BF16)
+        cross.append(
+            remote(sum_out.at[:, part], sum_in.at[:, part], cross_send.at[2 + n], cross_recv.at[2 + n], across)
+        )
+        cross[-1].start()
+    products(5, 8)
     sums["a"].wait_recv()
-    c_out[...] = (partial[3] + a_in[...].astype(F32)).astype(BF16)
+    c_out[...] = (partial[5] + a_in[...].astype(F32)).astype(BF16)
     sums["c0"].start()
     sums["c1"].start()
-    swaps[1].wait_recv()
-    sum_out[...] = (acc[quarter[2]] + acc_in[1]).astype(BF16)
-    sum_cross = remote(sum_out, sum_in, cross_send.at[2], cross_recv.at[2], across)
-    sum_cross.start()
     sums["b0"].wait_recv()
     sums["b1"].wait_recv()
-    d_out[...] = (partial[4] + b_in[0].astype(F32) + b_in[1].astype(F32)).astype(BF16)
+    d_out[...] = (partial[6] + b_in[0].astype(F32) + b_in[1].astype(F32)).astype(BF16)
     sums["d"].start()
     sums["c0"].wait_recv()
-    partial[5, lo] += c_in[lo].astype(F32)
-    e_out[0] = partial[5].astype(BF16)
+    e_out[0, lo] = (partial[3, lo] + c_in[lo].astype(F32)).astype(BF16)
     sums["e0"].start()
     sums["c1"].wait_recv()
-    partial[6, hi] += c_in[hi].astype(F32)
-    e_out[1] = partial[6].astype(BF16)
+    e_out[1, hi] = (partial[4, hi] + c_in[hi].astype(F32)).astype(BF16)
     sums["e1"].start()
 
     def finish(start, size):
@@ -349,15 +386,17 @@
         gate_out[here] = (total * up_slope[here]).astype(BF16)
 
     swaps[0].wait_recv()
-    sum_cross.wait_recv()
-    over_units(finish, 0, chunks)
+    cross[0].wait_recv()
+    over_units(finish, 0, 5)
+    cross[1].wait_recv()
+    over_units(finish, 5, chunks)
     sums["d"].wait_recv()
     down_out[...] = partial[7] + d_in[...].astype(F32)
-    sums["e0"].wait_recv()
-    sums["e1"].wait_recv()
+    for key in ("f0", "f1", "e0", "e1"):
+        sums[key].wait_recv()
     down_out[...] += e_in[0].astype(F32) + e_in[1].astype(F32)
 
-    for copy in (*sent, *crossing, *swaps, sum_cross, *sums.values()):
+    for copy in (*sent, *crossing, *weighing, *swaps, *cross, *sums.values()):
         copy.wait_send()
     for d in range(8):
         swap(d).wait_send()
@@ -406,13 +445,16 @@
         pltpu.VMEM((1, tokens), F32),
         pltpu.VMEM((1, tokens), F32),
         pltpu.VMEM((1, tokens), jnp.int32),
+        pltpu.VMEM((4 * tall, width), BF16),
+        pltpu.VMEM((8, tokens), F32),
+        pltpu.VMEM((3, 8, tokens), F32),
         pltpu.VMEM((8, rows, ff), F32),
         *(
             pltpu.VMEM((*lead, rows, ff), BF16)
             for lead in ((), (2,), (), (), (2,), (), (2,), (), (), (2,))
         ),
-        dma((7,)), dma((7,)), dma((7,)), dma((8,)), dma((8,)), dma((8,)), dma((8,)), dma((3,)), dma((3,)), dma((8,)), dma((8,)),
-        dma((3,)), dma((3,)), dma((4,)), dma((4,)), dma((8,)), dma((8,)),
+        dma((7,)), dma((7,)), dma((7,)), dma((8,)), dma((8,)), dma((8,)), dma((8,)), dma((4,)), dma((4,)), dma((8,)), dma((8,)),
+        dma((4,)), dma((4,)), dma((4,)), dma((4,)), dma((10,)), dma((10,)), dma((3,)), dma((3,)),
     ]
     outs = (
         jax.ShapeDtypeStruct((ff, tokens), BF16),

time: 55.8 us -> 53 us (0.950)
  Pallas kernels: 53.8 us -> 50.9 us
    pallas_call x1, Pallas kernels: 52.7 us -> 49.9 us  [local(): pl.pallas_call(functools.partial(kernel, rows, low), out_shape=tuple((plt...]
where the time goes in v5:
time: 53 us; the launch traced here: 52.9 us
  Pallas kernels  50.9 us (96%)
  between operations  1.93 us (4%)
    pallas_call x1, Pallas kernels, local(): pl.pallas_call(functools.partial(kernel, rows, low), out_shape=tuple((plt...  49.9 us

profile of v5, /device:TPU:1, one launch (start us, length us, event | category | flops | bytes accessed | tf_op | source)
XLA Modules:
  0.0 52.9 jit_solution(1677307178058535556)
XLA Ops:
  1.9 49.9 %shard_map.112 = (bf16[1344,128]{1,0:T(8,128)(2,1)S(1)}, bf16[1344,128]{1,0:T(8,128)(2,1)S(1)}, f32[84,1344]{1,0:T(8,128)S(1)}) custom-call(bf16[84,1344]{1,0:T(8,128)(2,1)} %weight.1, bf16[336,128]{1,0:T(8,128)(2,1)} %bitcast.10, bf16[1344,128]{1,0:T(8,128)(2,1)} %bitcast.8, bf16[1344,128]{1,0:T(8,128)(2,1)} %bitcast.9, f32[1,128]{1,0:T(1,128)} %bitcast.11, ...), custom_call_target="tpu_custom_call" | custom-call | tf_op jit(solution)/shard_map/pallas_call | solution.py:464
  51.8 1.0 %shard_map.113 = (bf16[1344,128]{1,0:T(8,128)(2,1)}, bf16[1344,128]{1,0:T(8,128)(2,1)}, f32[84,1344]{1,0:T(8,128)}) custom-call(bf16[1344,128]{1,0:T(8,128)(2,1)S(1)} %get-tuple-element.9.refs_0_, bf16[1344,128]{1,0:T(8,128)(2,1)S(1)} %get-tuple-element.10.refs_1_, f32[84,1344]{1,0:T(8,128)S(1)} %get-tuple-element.11.refs_2_), custom_call_target="tpu_custom_call" | custom-call | tf_op jit(solution)/shard_map/pallas_call | solution.py:476

commit v6 on v5

--- a/solution.py
+++ b/solution.py
@@ -385,13 +385,13 @@
         up_out[here] = (total * act[here]).astype(BF16)
         gate_out[here] = (total * up_slope[here]).astype(BF16)
 
+    sums["d"].wait_recv()
+    down_out[...] = partial[7] + d_in[...].astype(F32)
     swaps[0].wait_recv()
     cross[0].wait_recv()
     over_units(finish, 0, 5)
     cross[1].wait_recv()
     over_units(finish, 5, chunks)
-    sums["d"].wait_recv()
-    down_out[...] = partial[7] + d_in[...].astype(F32)
     for key in ("f0", "f1", "e0", "e1"):
         sums[key].wait_recv()
     down_out[...] += e_in[0].astype(F32) + e_in[1].astype(F32)

time: 53 us -> 53 us (level)
  no operation moved by 1% of the time
where the time goes in v6:
time: 53 us; the launch traced here: 52.9 us
  Pallas kernels  50.9 us (96%)
  between operations  1.93 us (4%)
    pallas_call x1, Pallas kernels, local(): pl.pallas_call(functools.partial(kernel, rows, low), out_shape=tuple((plt...  49.9 us

profile of v6, /device:TPU:1, one launch (start us, length us, event | category | flops | bytes accessed | tf_op | source)
XLA Modules:
  0.0 52.9 jit_solution(10917593141612739995)
XLA Ops:
  1.9 49.9 %shard_map.112 = (bf16[1344,128]{1,0:T(8,128)(2,1)S(1)}, bf16[1344,128]{1,0:T(8,128)(2,1)S(1)}, f32[84,1344]{1,0:T(8,128)S(1)}) custom-call(bf16[84,1344]{1,0:T(8,128)(2,1)} %weight.1, bf16[336,128]{1,0:T(8,128)(2,1)} %bitcast.10, bf16[1344,128]{1,0:T(8,128)(2,1)} %bitcast.8, bf16[1344,128]{1,0:T(8,128)(2,1)} %bitcast.9, f32[1,128]{1,0:T(1,128)} %bitcast.11, ...), custom_call_target="tpu_custom_call" | custom-call | tf_op jit(solution)/shard_map/pallas_call | solution.py:464
  51.8 1.0 %shard_map.113 = (bf16[1344,128]{1,0:T(8,128)(2,1)}, bf16[1344,128]{1,0:T(8,128)(2,1)}, f32[84,1344]{1,0:T(8,128)}) custom-call(bf16[1344,128]{1,0:T(8,128)(2,1)S(1)} %get-tuple-element.9.refs_0_, bf16[1344,128]{1,0:T(8,128)(2,1)S(1)} %get-tuple-element.10.refs_1_, f32[84,1344]{1,0:T(8,128)S(1)} %get-tuple-element.11.refs_2_), custom_call_target="tpu_custom_call" | custom-call | tf_op jit(solution)/shard_map/pallas_call | solution.py:476
